TPU v7x, 256 devices: a whole 4x4x8 slice. The times are simulated.
256 devices in a mesh: gx: 4 (over x), gy: 4 (over y), gz: 16 (over z, core).
Axes of the slice: x: 4, y: 4, z: 8, core: 2. Of those that a mesh axis runs over, the one named last changes fastest.
Arguments:
- residual: float32 [3, 256, 256, 512], P(None, 'gz', 'gx', 'gy'), may hold values from -32 to 32
- edge_diag: float32 [3, 256, 256, 512], P(None, 'gz', 'gx', 'gy'), may hold values from 6.5 to 9
- node_shift: float32 [256, 256, 512], P('gz', 'gx', 'gy'), may hold values from 0.05 to 3
- coarse_shift: float32 [128, 128, 256], P('gz', 'gx', 'gy'), may hold values from 0.05 to 3
Outputs:
- correction: float32 [3, 256, 256, 512], P(None, 'gz', 'gx', 'gy')
All inputs are finite; a program needn't handle non-finite values.
Results may differ from a plain program's by a relative error of at most 0.000021.
Values sent between devices are 32-bit elements; how exact they have to be, the bound alone decides.
A program may use at most 128 MiB of HBM per device.

v0:
```python
import jax
import jax.numpy as jnp
from jax import lax
from jax.sharding import Mesh
from jax.sharding import PartitionSpec as P

GX_GY_GZ = ("gx", "gy", "gz_0", "gz_1")
GZ = ("gz_0", "gz_1")


def extended(shard, sides, width):
    edges = {}
    for axis, dim in sides:
        size, length = (lax.axis_size(axis), shard.shape[dim])
        up = [(i, (i + 1) % size) for i in range(size - 1)]
        last = lax.slice_in_dim(shard, length - width, length, axis=dim)
        leading = lax.slice_in_dim(shard, 0, width, axis=dim)
        edges[dim] = (
            lax.ppermute(last, axis, up),
            lax.ppermute(leading, axis, [(b, a) for a, b in up]),
        )
    done = []
    for _, dim in sides:
        low, high = edges[dim]
        around = [(width, width) if d in done else (0, 0) for d in range(shard.ndim)]
        shard = jnp.concatenate([jnp.pad(low, around), shard, jnp.pad(high, around)], axis=dim)
        done.append(dim)
    return shard


def by_axis(shard, axes):
    for axis in axes:
        shard = lax.psum(shard, axis)
    return shard


def neighbours(padded):
    total = padded[2:, 1:-1, 1:-1] + padded[:-2, 1:-1, 1:-1]
    total = total + padded[1:-1, 2:, 1:-1] + padded[1:-1, :-2, 1:-1]
    return total + padded[1:-1, 1:-1, 2:] + padded[1:-1, 1:-1, :-2]


def node_faces(field):
    return extended(field, (("gx", 1), ("gy", 2), (GZ, 0)), 1)


def coarse_faces(field):
    return extended(field, (("gx", 1), ("gy", 2), (GZ, 0)), 1)


def apply_padded(padded, diagonal):
    return diagonal * padded[1:-1, 1:-1, 1:-1] - neighbours(padded)


def local(residual, edge_diag, node_shift, coarse_shift):
    joined = jnp.concatenate((residual, edge_diag), axis=0)
    padded_both = extended(joined, (("gx", 2), ("gy", 3), (GZ, 1)), 1)
    padded_diag = padded_both[3:]
    padded = padded_both[:3] / jnp.where(padded_diag > 0.0, padded_diag, 1.0)
    scaled = padded[:, 1:-1, 1:-1, 1:-1]
    edge_near = jnp.stack([neighbours(padded[component]) for component in range(3)])
    smooth_part = 2.0 * scaled - (edge_diag * scaled - edge_near) / edge_diag
    nodal_rhs = (
        padded[0, :-2, 1:-1, 1:-1]
        - scaled[0]
        + (padded[1, 1:-1, :-2, 1:-1] - scaled[1])
        + (padded[2, 1:-1, 1:-1, :-2] - scaled[2])
    )
    node_diag = 6.0 + node_shift
    first_guess = nodal_rhs / node_diag
    node_res = nodal_rhs - apply_padded(node_faces(first_guess), node_diag)
    sx, sy, sz = node_res.shape
    coarse_rhs = node_res.reshape(sx // 2, 2, sy // 2, 2, sz // 2, 2).sum(axis=(1, 3, 5))
    coarse_diag = 6.0 + coarse_shift
    first_dir = coarse_rhs / coarse_diag
    first_image = apply_padded(coarse_faces(first_dir), coarse_diag)
    second_dir = first_image / coarse_diag
    second_image = apply_padded(coarse_faces(second_dir), coarse_diag)
    gone, gtwo, hone, hmix, htwo = (
        by_axis(jnp.sum(first_dir * coarse_rhs), GX_GY_GZ),
        by_axis(jnp.sum(second_dir * coarse_rhs), GX_GY_GZ),
        by_axis(jnp.sum(first_dir * first_image), GX_GY_GZ),
        by_axis(jnp.sum(second_dir * first_image), GX_GY_GZ),
        by_axis(jnp.sum(second_dir * second_image), GX_GY_GZ),
    )
    coef_two = (gtwo - hmix * gone / hone) / (htwo - hmix * hmix / hone)
    coef_one = (gone - hmix * coef_two) / hone
    coarse_sol = coef_one * first_dir + coef_two * second_dir
    spread = jnp.broadcast_to(
        coarse_sol[:, None, :, None, :, None], (sx // 2, 2, sy // 2, 2, sz // 2, 2)
    ).reshape(sx, sy, sz)
    nodal = first_guess + spread
    final_nodal = nodal + (nodal_rhs - apply_padded(node_faces(nodal), node_diag)) / node_diag
    fpad = node_faces(final_nodal)
    grads = jnp.stack(
        [
            fpad[2:, 1:-1, 1:-1] - final_nodal,
            fpad[1:-1, 2:, 1:-1] - final_nodal,
            fpad[1:-1, 1:-1, 2:] - final_nodal,
        ]
    )
    return smooth_part + grads


def solution(mesh):
    torus = Mesh(
        mesh.devices.reshape(mesh.shape["gx"], mesh.shape["gy"], 8, 2), ("gx", "gy", "gz_0", "gz_1")
    )
    return jax.shard_map(
        local,
        mesh=torus,
        in_specs=(
            P(None, GZ, "gx", "gy"),
            P(None, GZ, "gx", "gy"),
            P(GZ, "gx", "gy"),
            P(GZ, "gx", "gy"),
        ),
        out_specs=P(None, GZ, "gx", "gy"),
        check_vma=False,
    )
```

profile of v0, /device:TPU:1, one launch (start us, length us, event | category | flops | bytes accessed | tf_op | source)
XLA Modules:
  0.0 298.0 jit_solution(11723002952355551549)
XLA Ops:
  2.1 3.7 %fusion.67 = (f32[6,16,64,1]{3,2,1,0:T(8,128)}, f32[6,16,64,1]{3,2,1,0:T(8,128)}) fusion(f32[6,16,64,128]{3,2,1,0:T(8,128)S(1)} %constant_dynamic-update-slice_fusion), kind=kLoop, calls=%fused_computation.194 | loop fusion | bytes 98304 | tf_op jit(solution)/shard_map/slice | solution.py:16
  5.7 3.1 %copy.5 = f32[6,16,64,1]{2,1,3,0:T(8,128)} copy(f32[6,16,64,1]{3,2,1,0:T(8,128)} %get-tuple-element.39) | data formatting | bytes 49152 | tf_op jit(solution)/shard_map/slice | solution.py:16
  8.8 4.6 %collective-permute-start.1 = (f32[6,16,64,1]{2,1,3,0:T(8,128)}, f32[6,16,64,1]{2,1,3,0:T(8,128)}, u32[]{:S(2)}, u32[]{:S(2)}) collective-permute-start(f32[6,16,64,1]{2,1,3,0:T(8,128)} %copy.5), channel_id=1, source_target_pairs={{0,16},{16,32},{32,48},{1,17},{17,33},{33,49},{2,18},{18,34},{34,5... | collective-permute-start | bytes 73736 | tf_op jit(solution)/shard_map/ppermute | solution.py:19
  14.2 4.4 %collective-permute-start = (f32[6,1,64,128]{3,2,1,0:T(8,128)}, f32[6,1,64,128]{3,2,1,0:T(8,128)S(1)}, u32[]{:S(2)}, u32[]{:S(2)}) collective-permute-start(f32[6,1,64,128]{3,2,1,0:T(8,128)} %get-tuple-element.37), channel_id=1, source_target_pairs={{0,1},{1,2},{2,3},{3,4},{4,5},{5,6},{6,7},{7,8},{8,9},{9,10},{10,1... | collective-permute-start | bytes 589832 | tf_op jit(solution)/shard_map/ppermute | solution.py:19
  21.2 3.7 %collective-permute-start.2 = (f32[6,16,1,128]{3,2,1,0:T(1,128)}, f32[6,16,1,128]{3,2,1,0:T(1,128)}, u32[]{:S(2)}, u32[]{:S(2)}) collective-permute-start(f32[6,16,1,128]{3,2,1,0:T(1,128)} %get-tuple-element.35), channel_id=1, source_target_pairs={{0,64},{64,128},{128,192},{1,65},{65,129},{129,193},{2,66},{66,130... | collective-permute-start | bytes 147464 | tf_op jit(solution)/shard_map/ppermute | solution.py:19
  26.2 3.1 %copy.7 = f32[6,16,64,1]{2,1,3,0:T(8,128)} copy(f32[6,16,64,1]{3,2,1,0:T(8,128)} %get-tuple-element.40) | data formatting | bytes 49152 | tf_op jit(solution)/shard_map/slice | solution.py:17
  34.4 3.0 %copy.8 = f32[6,16,64,1]{3,2,1,0:T(8,128)} copy(f32[6,16,64,1]{2,1,3,0:T(8,128)} %collective-permute-done.4) | data formatting | bytes 49152 | tf_op jit(solution)/shard_map/ppermute | solution.py:20
  37.5 7.0 %select_maximum_fusion = f32[6,18,66,130]{3,2,1,0:T(8,128)S(1)} fusion(f32[6,1,64,128]{3,2,1,0:T(8,128)S(1)} %collective-permute-done.5, f32[6,16,64,1]{3,2,1,0:T(8,128)} %copy.8, f32[6,16,64,1]{3,2,1,0:T(8,128)} %copy.6, f32[6,1,64,128]{3,2,1,0:T(8,128)S(1)} %collective-permute-done, f32[6,16,1,128]{3,2,1,0:T(1,128)} %collective-permute-done.3, ...), kind=kLoop, calls=%fused_computation.3 | loop fusion | flops 19459440 | bytes 7392960 | tf_op jit(solution)/shard_map/concatenate | solution.py:26
  47.5 3.2 %collective-permute-start.6 = (f32[16,64,1]{2,1,0:T(8,128)S(1)}, f32[16,64,1]{2,1,0:T(8,128)S(1)}, u32[]{:S(2)}, u32[]{:S(2)}) collective-permute-start(f32[16,64,1]{2,1,0:T(8,128)S(1)} %get-tuple-element.57), channel_id=1, source_target_pairs={{0,16},{16,32},{32,48},{1,17},{17,33},{33,49},{2,18},{18,34},{34,5... | collective-permute-start | bytes 12296 | tf_op jit(solution)/shard_map/ppermute | solution.py:19
  52.6 4.8 %collective-permute-start.11 = (f32[1,64,128]{2,1,0:T(8,128)S(1)}, f32[1,64,128]{2,1,0:T(8,128)S(1)}, u32[]{:S(2)}, u32[]{:S(2)}) collective-permute-start(f32[1,64,128]{2,1,0:T(8,128)S(1)} %get-tuple-element.55), channel_id=1, source_target_pairs={{0,1},{1,2},{2,3},{3,4},{4,5},{5,6},{6,7},{7,8},{8,9},{9,10},{10,1... | collective-permute-start | bytes 98312 | tf_op jit(solution)/shard_map/ppermute | solution.py:19
  57.5 4.3 %collective-permute-start.7 = (f32[16,1,128]{2,1,0:T(1,128)S(1)}, f32[16,1,128]{2,1,0:T(1,128)S(1)}, u32[]{:S(2)}, u32[]{:S(2)}) collective-permute-start(f32[16,1,128]{2,1,0:T(1,128)S(1)} %get-tuple-element.58), channel_id=1, source_target_pairs={{0,64},{64,128},{128,192},{1,65},{65,129},{129,193},{2,66},{66,130... | collective-permute-start | bytes 24584 | tf_op jit(solution)/shard_map/ppermute | solution.py:19
  64.4 12.3 %collective-permute-done.9 = f32[16,64,1]{2,1,0:T(8,128)S(1)} collective-permute-done((f32[16,64,1]{2,1,0:T(8,128)S(1)}, f32[16,64,1]{2,1,0:T(8,128)S(1)}, u32[]{:S(2)}, u32[]{:S(2)}) %collective-permute-start.9) | collective-permute-done | bytes 4128 | tf_op jit(solution)/shard_map/ppermute | solution.py:20
  77.7 34.9 %reshape.12 = f32[8,2,32,2,64,2]{5,4,3,2,1,0:T(8,128)} reshape(f32[16,64,128]{2,1,0:T(8,128)S(1)} %fusion.30) | data formatting | bytes 1048576 | tf_op jit(solution)/shard_map/reshape | solution.py:73
  112.5 12.2 %reduce_sum.54 = f32[8,32,64]{2,1,0:T(8,128)S(1)} reduce(f32[8,2,32,2,64,2]{5,4,3,2,1,0:T(8,128)} %reshape.12, f32[]{:T(128)} %constant.4.clone.1), dimensions={1,3,5}, to_apply=%region_0.1 | reduce | flops 114688 | bytes 589828 | tf_op jit(solution)/shard_map/reduce_sum | solution.py:73
  125.0 3.6 %collective-permute-start.12 = (f32[8,32,1]{2,1,0:T(8,128)S(1)}, f32[8,32,1]{2,1,0:T(8,128)S(1)}, u32[]{:S(2)}, u32[]{:S(2)}) collective-permute-start(f32[8,32,1]{2,1,0:T(8,128)S(1)} %get-tuple-element.69), channel_id=1, source_target_pairs={{0,16},{16,32},{32,48},{1,17},{17,33},{33,49},{2,18},{18,34},{34,5... | collective-permute-start | bytes 3080 | tf_op jit(solution)/shard_map/ppermute | solution.py:19
  130.5 5.5 %collective-permute-start.17 = (f32[1,32,64]{2,1,0:T(8,128)S(1)}, f32[1,32,64]{2,1,0:T(8,128)S(1)}, u32[]{:S(2)}, u32[]{:S(2)}) collective-permute-start(f32[1,32,64]{2,1,0:T(8,128)S(1)} %get-tuple-element.67), channel_id=1, source_target_pairs={{0,1},{1,2},{2,3},{3,4},{4,5},{5,6},{6,7},{7,8},{8,9},{9,10},{10,1... | collective-permute-start | bytes 24584 | tf_op jit(solution)/shard_map/ppermute | solution.py:19
  136.0 4.0 %collective-permute-start.13 = (f32[8,1,64]{2,1,0:T(1,128)S(1)}, f32[8,1,64]{2,1,0:T(1,128)S(1)}, u32[]{:S(2)}, u32[]{:S(2)}) collective-permute-start(f32[8,1,64]{2,1,0:T(1,128)S(1)} %get-tuple-element.70), channel_id=1, source_target_pairs={{0,64},{64,128},{128,192},{1,65},{65,129},{129,193},{2,66},{66,130... | collective-permute-start | bytes 6152 | tf_op jit(solution)/shard_map/ppermute | solution.py:19
  142.7 4.5 %collective-permute-done.15 = f32[8,32,1]{2,1,0:T(8,128)S(1)} collective-permute-done((f32[8,32,1]{2,1,0:T(8,128)S(1)}, f32[8,32,1]{2,1,0:T(8,128)S(1)}, u32[]{:S(2)}, u32[]{:S(2)}) %collective-permute-start.15) | collective-permute-done | bytes 1056 | tf_op jit(solution)/shard_map/ppermute | solution.py:20
  148.3 3.6 %collective-permute-start.18 = (f32[8,32,1]{2,1,0:T(8,128)S(1)}, f32[8,32,1]{2,1,0:T(8,128)S(1)}, u32[]{:S(2)}, u32[]{:S(2)}) collective-permute-start(f32[8,32,1]{2,1,0:T(8,128)S(1)} %get-tuple-element.63), channel_id=1, source_target_pairs={{0,16},{16,32},{32,48},{1,17},{17,33},{33,49},{2,18},{18,34},{34,5... | collective-permute-start | bytes 3080 | tf_op jit(solution)/shard_map/ppermute | solution.py:19
  155.5 4.1 %collective-permute-start.23 = (f32[1,32,64]{2,1,0:T(8,128)S(1)}, f32[1,32,64]{2,1,0:T(8,128)S(1)}, u32[]{:S(2)}, u32[]{:S(2)}) collective-permute-start(f32[1,32,64]{2,1,0:T(8,128)S(1)} %get-tuple-element.61), channel_id=1, source_target_pairs={{0,1},{1,2},{2,3},{3,4},{4,5},{5,6},{6,7},{7,8},{8,9},{9,10},{10,1... | collective-permute-start | bytes 24584 | tf_op jit(solution)/shard_map/ppermute | solution.py:19
  159.6 4.5 %collective-permute-start.19 = (f32[8,1,64]{2,1,0:T(1,128)S(1)}, f32[8,1,64]{2,1,0:T(1,128)S(1)}, u32[]{:S(2)}, u32[]{:S(2)}) collective-permute-start(f32[8,1,64]{2,1,0:T(1,128)S(1)} %get-tuple-element.64), channel_id=1, source_target_pairs={{0,64},{64,128},{128,192},{1,65},{65,129},{129,193},{2,66},{66,130... | collective-permute-start | bytes 6152 | tf_op jit(solution)/shard_map/ppermute | solution.py:19
  165.6 3.5 %slice_bitcast_fusion.2 = (f32[18,66,130]{2,1,0:T(8,128)}, f32[18,66,130]{2,1,0:T(8,128)S(1)}, f32[18,66,130]{2,1,0:T(8,128)S(1)}) fusion(f32[3,18,66,130]{3,2,1,0:T(8,128)} %copy-done), kind=kLoop, calls=%fused_computation.21 | loop fusion | bytes 3706560 | tf_op jit(solution)/shard_map/squeeze | solution.py:61
  170.2 10.0 %all-reduce.25 = (f32[]{:T(128)}, f32[]{:T(128)}, f32[]{:T(128)}, f32[]{:T(128)}, f32[]{:T(128)}) all-reduce(f32[]{:T(128)} %get-tuple-element.7, f32[]{:T(128)} %get-tuple-element.6, f32[]{:T(128)} %get-tuple-element.8, f32[]{:T(128)} %get-tuple-element.5, f32[]{:T(128)} %fusion.49), channel_id=1, replica_groups=mesh['gx'=4,'gy'=4,'gz_0'=8,'gz_1'=2] {'gx'}, use_global_device_ids=true, to_apply=%region_12.13 | all-reduce | flops 5 | bytes 40 | tf_op jit(solution)/shard_map/psum | solution.py:33
  180.2 9.0 %all-reduce.24 = (f32[]{:T(128)}, f32[]{:T(128)}, f32[]{:T(128)}, f32[]{:T(128)}, f32[]{:T(128)}) all-reduce(f32[]{:T(128)} %get-tuple-element.19, f32[]{:T(128)} %get-tuple-element.20, f32[]{:T(128)} %get-tuple-element.21, f32[]{:T(128)} %get-tuple-element.22, ...), channel_id=1, replica_groups=mesh['gx'=4,'gy'=4,'gz_0'=8,'gz_1'=2] {'gy'}, use_global_device_ids=true, to_apply=%region_13.14 | all-reduce | flops 5 | bytes 40 | tf_op jit(solution)/shard_map/psum | solution.py:33
  189.3 16.5 %all-reduce.23 = (f32[]{:T(128)}, f32[]{:T(128)}, f32[]{:T(128)}, f32[]{:T(128)}, f32[]{:T(128)}) all-reduce(f32[]{:T(128)} %get-tuple-element.14, f32[]{:T(128)} %get-tuple-element.15, f32[]{:T(128)} %get-tuple-element.16, f32[]{:T(128)} %get-tuple-element.17, ...), channel_id=1, replica_groups=mesh['gx'=4,'gy'=4,'gz_0'=8,'gz_1'=2] {'gz_0'}, use_global_device_ids=true, to_apply=%region_14.15 | all-reduce | flops 5 | bytes 40 | tf_op jit(solution)/shard_map/psum | solution.py:33
  205.8 9.6 %all-reduce.26 = (f32[]{:T(128)}, f32[]{:T(128)}, f32[]{:T(128)}, f32[]{:T(128)}, f32[]{:T(128)}) all-reduce(f32[]{:T(128)} %get-tuple-element.9, f32[]{:T(128)} %get-tuple-element.10, f32[]{:T(128)} %get-tuple-element.11, f32[]{:T(128)} %get-tuple-element.12, ...), channel_id=1, replica_groups=mesh['gx'=4,'gy'=4,'gz_0'=8,'gz_1'=2] {'gz_1'}, use_global_device_ids=true, to_apply=%region_15.16 | all-reduce | flops 5 | bytes 40 | tf_op jit(solution)/shard_map/psum | solution.py:33
  222.0 11.4 %broadcast_in_dim.11 = f32[8,2,32,2,64,2]{5,4,3,2,1,0:T(8,128)} broadcast(f32[8,32,64]{2,1,0:T(8,128)S(1)} %multiply_add_fusion), dimensions={0,2,4} | broadcast | bytes 589824 | tf_op jit(solution)/shard_map/broadcast_in_dim | solution.py:89
  233.4 24.4 %reshape.13 = f32[16,64,128]{2,1,0:T(8,128)} reshape(f32[8,2,32,2,64,2]{5,4,3,2,1,0:T(8,128)} %broadcast_in_dim.11) | data formatting | bytes 1048576 | tf_op jit(solution)/shard_map/reshape | solution.py:91
  264.1 3.3 %collective-permute-start.29 = (f32[1,64,128]{2,1,0:T(8,128)S(1)}, f32[1,64,128]{2,1,0:T(8,128)S(1)}, u32[]{:S(2)}, u32[]{:S(2)}) collective-permute-start(f32[1,64,128]{2,1,0:T(8,128)S(1)} %get-tuple-element.49), channel_id=1, source_target_pairs={{0,1},{1,2},{2,3},{3,4},{4,5},{5,6},{6,7},{7,8},{8,9},{9,10},{10,1... | collective-permute-start | bytes 98312 | tf_op jit(solution)/shard_map/ppermute | solution.py:19
  278.7 4.5 %collective-permute-start.30 = (f32[16,64,1]{2,1,0:T(8,128)S(1)}, f32[16,64,1]{2,1,0:T(8,128)S(1)}, u32[]{:S(2)}, u32[]{:S(2)}) collective-permute-start(f32[16,64,1]{2,1,0:T(8,128)S(1)} %get-tuple-element.44), channel_id=1, source_target_pairs={{0,16},{16,32},{32,48},{1,17},{17,33},{33,49},{2,18},{18,34},{34,5... | collective-permute-start | bytes 12296 | tf_op jit(solution)/shard_map/ppermute | solution.py:19
  283.1 4.3 %collective-permute-start.34 = (f32[1,64,128]{2,1,0:T(8,128)S(1)}, f32[1,64,128]{2,1,0:T(8,128)S(1)}, u32[]{:S(2)}, u32[]{:S(2)}) collective-permute-start(f32[1,64,128]{2,1,0:T(8,128)S(1)} %slice.462), channel_id=1, source_target_pairs={{1,0},{2,1},{3,2},{4,3},{5,4},{6,5},{7,6},{8,7},{9,8},{10,9},{11,1... | collective-permute-start | bytes 98312 | tf_op jit(solution)/shard_map/ppermute | solution.py:20
  294.0 4.0 %fusion.7 = f32[3,16,64,128]{3,2,1,0:T(8,128)} fusion(f32[3,16,64,128]{3,2,1,0:T(8,128)S(1)} %copy-done.3, f32[1,16,64,128]{3,2,1,0:T(8,128)S(1)} %get-tuple-element.72, f32[1,16,64,128]{3,2,1,0:T(8,128)S(1)} %get-tuple-element.73, f32[1,16,64,128]{3,2,1,0:T(8,128)S(1)} %fusion.45, f32[1,16,64,128]{3,2,1,0:T(8,128)S(1)} %get-tuple-element.42, ...), kind=kLoop, calls=%fused_computation.18 | loop fusion | flops 3932160 | bytes 7864320 | tf_op jit(solution)/shard_map/add | solution.py:102
  (114 shorter events, 56.1 us)
Async XLA Ops:
  8.8 20.5 %collective-permute-start.1 = (f32[6,16,64,1]{2,1,3,0:T(8,128)}, f32[6,16,64,1]{2,1,3,0:T(8,128)}, u32[]{:S(2)}, u32[]{:S(2)}) collective-permute-start(f32[6,16,64,1]{2,1,3,0:T(8,128)} %copy.5), channel_id=1, source_target_pairs={{0,16},{16,32},{32,48},{1,17},{17,33},{33,49},{2,18},{18,34},{34,5... | collective-permute-start | bytes 73736 | tf_op jit(solution)/shard_map/ppermute | solution.py:19
  14.2 23.3 %collective-permute-start = (f32[6,1,64,128]{3,2,1,0:T(8,128)}, f32[6,1,64,128]{3,2,1,0:T(8,128)S(1)}, u32[]{:S(2)}, u32[]{:S(2)}) collective-permute-start(f32[6,1,64,128]{3,2,1,0:T(8,128)} %get-tuple-element.37), channel_id=1, source_target_pairs={{0,1},{1,2},{2,3},{3,4},{4,5},{5,6},{6,7},{7,8},{8,9},{9,10},{10,1... | collective-permute-start | bytes 589832 | tf_op jit(solution)/shard_map/ppermute | solution.py:19
  18.6 18.9 %collective-permute-start.5 = (f32[6,1,64,128]{3,2,1,0:T(8,128)}, f32[6,1,64,128]{3,2,1,0:T(8,128)S(1)}, u32[]{:S(2)}, u32[]{:S(2)}) collective-permute-start(f32[6,1,64,128]{3,2,1,0:T(8,128)} %get-tuple-element.38), channel_id=1, source_target_pairs={{1,0},{2,1},{3,2},{4,3},{5,4},{6,5},{7,6},{8,7},{9,8},{10,9},{11,1... | collective-permute-start | bytes 589832 | tf_op jit(solution)/shard_map/ppermute | solution.py:20
  21.2 16.3 %collective-permute-start.2 = (f32[6,16,1,128]{3,2,1,0:T(1,128)}, f32[6,16,1,128]{3,2,1,0:T(1,128)}, u32[]{:S(2)}, u32[]{:S(2)}) collective-permute-start(f32[6,16,1,128]{3,2,1,0:T(1,128)} %get-tuple-element.35), channel_id=1, source_target_pairs={{0,64},{64,128},{128,192},{1,65},{65,129},{129,193},{2,66},{66,130... | collective-permute-start | bytes 147464 | tf_op jit(solution)/shard_map/ppermute | solution.py:19
  24.9 12.5 %collective-permute-start.3 = (f32[6,16,1,128]{3,2,1,0:T(1,128)}, f32[6,16,1,128]{3,2,1,0:T(1,128)}, u32[]{:S(2)}, u32[]{:S(2)}) collective-permute-start(f32[6,16,1,128]{3,2,1,0:T(1,128)} %get-tuple-element.36), channel_id=1, source_target_pairs={{64,0},{128,64},{192,128},{65,1},{129,65},{193,129},{66,2},{130,66... | collective-permute-start | bytes 147464 | tf_op jit(solution)/shard_map/ppermute | solution.py:20
  29.3 5.1 %collective-permute-start.4 = (f32[6,16,64,1]{2,1,3,0:T(8,128)}, f32[6,16,64,1]{2,1,3,0:T(8,128)}, u32[]{:S(2)}, u32[]{:S(2)}) collective-permute-start(f32[6,16,64,1]{2,1,3,0:T(8,128)} %copy.7), channel_id=1, source_target_pairs={{16,0},{32,16},{48,32},{17,1},{33,17},{49,33},{18,2},{34,18},{50,3... | collective-permute-start | bytes 73736 | tf_op jit(solution)/shard_map/ppermute | solution.py:20
  47.5 15.5 %collective-permute-start.6 = (f32[16,64,1]{2,1,0:T(8,128)S(1)}, f32[16,64,1]{2,1,0:T(8,128)S(1)}, u32[]{:S(2)}, u32[]{:S(2)}) collective-permute-start(f32[16,64,1]{2,1,0:T(8,128)S(1)} %get-tuple-element.57), channel_id=1, source_target_pairs={{0,16},{16,32},{32,48},{1,17},{17,33},{33,49},{2,18},{18,34},{34,5... | collective-permute-start | bytes 12296 | tf_op jit(solution)/shard_map/ppermute | solution.py:19
  50.7 26.2 %collective-permute-start.10 = (f32[1,64,128]{2,1,0:T(8,128)S(1)}, f32[1,64,128]{2,1,0:T(8,128)S(1)}, u32[]{:S(2)}, u32[]{:S(2)}) collective-permute-start(f32[1,64,128]{2,1,0:T(8,128)S(1)} %get-tuple-element.54), channel_id=1, source_target_pairs={{1,0},{2,1},{3,2},{4,3},{5,4},{6,5},{7,6},{8,7},{9,8},{10,9},{11,1... | collective-permute-start | bytes 98312 | tf_op jit(solution)/shard_map/ppermute | solution.py:20
  52.6 24.2 %collective-permute-start.11 = (f32[1,64,128]{2,1,0:T(8,128)S(1)}, f32[1,64,128]{2,1,0:T(8,128)S(1)}, u32[]{:S(2)}, u32[]{:S(2)}) collective-permute-start(f32[1,64,128]{2,1,0:T(8,128)S(1)} %get-tuple-element.55), channel_id=1, source_target_pairs={{0,1},{1,2},{2,3},{3,4},{4,5},{5,6},{6,7},{7,8},{8,9},{9,10},{10,1... | collective-permute-start | bytes 98312 | tf_op jit(solution)/shard_map/ppermute | solution.py:19
  57.5 19.4 %collective-permute-start.7 = (f32[16,1,128]{2,1,0:T(1,128)S(1)}, f32[16,1,128]{2,1,0:T(1,128)S(1)}, u32[]{:S(2)}, u32[]{:S(2)}) collective-permute-start(f32[16,1,128]{2,1,0:T(1,128)S(1)} %get-tuple-element.58), channel_id=1, source_target_pairs={{0,64},{64,128},{128,192},{1,65},{65,129},{129,193},{2,66},{66,130... | collective-permute-start | bytes 24584 | tf_op jit(solution)/shard_map/ppermute | solution.py:19
  61.8 15.1 %collective-permute-start.8 = (f32[16,1,128]{2,1,0:T(1,128)S(1)}, f32[16,1,128]{2,1,0:T(1,128)S(1)}, u32[]{:S(2)}, u32[]{:S(2)}) collective-permute-start(f32[16,1,128]{2,1,0:T(1,128)S(1)} %get-tuple-element.59), channel_id=1, source_target_pairs={{64,0},{128,64},{192,128},{65,1},{129,65},{193,129},{66,2},{130,66... | collective-permute-start | bytes 24584 | tf_op jit(solution)/shard_map/ppermute | solution.py:20
  63.1 13.7 %collective-permute-start.9 = (f32[16,64,1]{2,1,0:T(8,128)S(1)}, f32[16,64,1]{2,1,0:T(8,128)S(1)}, u32[]{:S(2)}, u32[]{:S(2)}) collective-permute-start(f32[16,64,1]{2,1,0:T(8,128)S(1)} %get-tuple-element.56), channel_id=1, source_target_pairs={{16,0},{32,16},{48,32},{17,1},{33,17},{49,33},{18,2},{34,18},{50,3... | collective-permute-start | bytes 12296 | tf_op jit(solution)/shard_map/ppermute | solution.py:20
  125.0 16.4 %collective-permute-start.12 = (f32[8,32,1]{2,1,0:T(8,128)S(1)}, f32[8,32,1]{2,1,0:T(8,128)S(1)}, u32[]{:S(2)}, u32[]{:S(2)}) collective-permute-start(f32[8,32,1]{2,1,0:T(8,128)S(1)} %get-tuple-element.69), channel_id=1, source_target_pairs={{0,16},{16,32},{32,48},{1,17},{17,33},{33,49},{2,18},{18,34},{34,5... | collective-permute-start | bytes 3080 | tf_op jit(solution)/shard_map/ppermute | solution.py:19
  128.6 18.6 %collective-permute-start.16 = (f32[1,32,64]{2,1,0:T(8,128)S(1)}, f32[1,32,64]{2,1,0:T(8,128)S(1)}, u32[]{:S(2)}, u32[]{:S(2)}) collective-permute-start(f32[1,32,64]{2,1,0:T(8,128)S(1)} %get-tuple-element.66), channel_id=1, source_target_pairs={{1,0},{2,1},{3,2},{4,3},{5,4},{6,5},{7,6},{8,7},{9,8},{10,9},{11,1... | collective-permute-start | bytes 24584 | tf_op jit(solution)/shard_map/ppermute | solution.py:20
  130.5 16.7 %collective-permute-start.17 = (f32[1,32,64]{2,1,0:T(8,128)S(1)}, f32[1,32,64]{2,1,0:T(8,128)S(1)}, u32[]{:S(2)}, u32[]{:S(2)}) collective-permute-start(f32[1,32,64]{2,1,0:T(8,128)S(1)} %get-tuple-element.67), channel_id=1, source_target_pairs={{0,1},{1,2},{2,3},{3,4},{4,5},{5,6},{6,7},{7,8},{8,9},{9,10},{10,1... | collective-permute-start | bytes 24584 | tf_op jit(solution)/shard_map/ppermute | solution.py:19
  136.0 11.1 %collective-permute-start.13 = (f32[8,1,64]{2,1,0:T(1,128)S(1)}, f32[8,1,64]{2,1,0:T(1,128)S(1)}, u32[]{:S(2)}, u32[]{:S(2)}) collective-permute-start(f32[8,1,64]{2,1,0:T(1,128)S(1)} %get-tuple-element.70), channel_id=1, source_target_pairs={{0,64},{64,128},{128,192},{1,65},{65,129},{129,193},{2,66},{66,130... | collective-permute-start | bytes 6152 | tf_op jit(solution)/shard_map/ppermute | solution.py:19
  140.0 7.1 %collective-permute-start.14 = (f32[8,1,64]{2,1,0:T(1,128)S(1)}, f32[8,1,64]{2,1,0:T(1,128)S(1)}, u32[]{:S(2)}, u32[]{:S(2)}) collective-permute-start(f32[8,1,64]{2,1,0:T(1,128)S(1)} %get-tuple-element.71), channel_id=1, source_target_pairs={{64,0},{128,64},{192,128},{65,1},{129,65},{193,129},{66,2},{130,66... | collective-permute-start | bytes 6152 | tf_op jit(solution)/shard_map/ppermute | solution.py:20
  141.3 5.8 %collective-permute-start.15 = (f32[8,32,1]{2,1,0:T(8,128)S(1)}, f32[8,32,1]{2,1,0:T(8,128)S(1)}, u32[]{:S(2)}, u32[]{:S(2)}) collective-permute-start(f32[8,32,1]{2,1,0:T(8,128)S(1)} %get-tuple-element.68), channel_id=1, source_target_pairs={{16,0},{32,16},{48,32},{17,1},{33,17},{49,33},{18,2},{34,18},{50,3... | collective-permute-start | bytes 3080 | tf_op jit(solution)/shard_map/ppermute | solution.py:20
  148.3 15.8 %collective-permute-start.18 = (f32[8,32,1]{2,1,0:T(8,128)S(1)}, f32[8,32,1]{2,1,0:T(8,128)S(1)}, u32[]{:S(2)}, u32[]{:S(2)}) collective-permute-start(f32[8,32,1]{2,1,0:T(8,128)S(1)} %get-tuple-element.63), channel_id=1, source_target_pairs={{0,16},{16,32},{32,48},{1,17},{17,33},{33,49},{2,18},{18,34},{34,5... | collective-permute-start | bytes 3080 | tf_op jit(solution)/shard_map/ppermute | solution.py:19
  151.9 17.3 %collective-permute-start.21 = (f32[8,32,1]{2,1,0:T(8,128)S(1)}, f32[8,32,1]{2,1,0:T(8,128)S(1)}, u32[]{:S(2)}, u32[]{:S(2)}) collective-permute-start(f32[8,32,1]{2,1,0:T(8,128)S(1)} %get-tuple-element.62), channel_id=1, source_target_pairs={{16,0},{32,16},{48,32},{17,1},{33,17},{49,33},{18,2},{34,18},{50,3... | collective-permute-start | bytes 3080 | tf_op jit(solution)/shard_map/ppermute | solution.py:20
  153.2 16.0 %collective-permute-start.22 = (f32[1,32,64]{2,1,0:T(8,128)S(1)}, f32[1,32,64]{2,1,0:T(8,128)S(1)}, u32[]{:S(2)}, u32[]{:S(2)}) collective-permute-start(f32[1,32,64]{2,1,0:T(8,128)S(1)} %get-tuple-element.60), channel_id=1, source_target_pairs={{1,0},{2,1},{3,2},{4,3},{5,4},{6,5},{7,6},{8,7},{9,8},{10,9},{11,1... | collective-permute-start | bytes 24584 | tf_op jit(solution)/shard_map/ppermute | solution.py:20
  155.5 13.8 %collective-permute-start.23 = (f32[1,32,64]{2,1,0:T(8,128)S(1)}, f32[1,32,64]{2,1,0:T(8,128)S(1)}, u32[]{:S(2)}, u32[]{:S(2)}) collective-permute-start(f32[1,32,64]{2,1,0:T(8,128)S(1)} %get-tuple-element.61), channel_id=1, source_target_pairs={{0,1},{1,2},{2,3},{3,4},{4,5},{5,6},{6,7},{7,8},{8,9},{9,10},{10,1... | collective-permute-start | bytes 24584 | tf_op jit(solution)/shard_map/ppermute | solution.py:19
  159.6 9.6 %collective-permute-start.19 = (f32[8,1,64]{2,1,0:T(1,128)S(1)}, f32[8,1,64]{2,1,0:T(1,128)S(1)}, u32[]{:S(2)}, u32[]{:S(2)}) collective-permute-start(f32[8,1,64]{2,1,0:T(1,128)S(1)} %get-tuple-element.64), channel_id=1, source_target_pairs={{0,64},{64,128},{128,192},{1,65},{65,129},{129,193},{2,66},{66,130... | collective-permute-start | bytes 6152 | tf_op jit(solution)/shard_map/ppermute | solution.py:19
  164.2 5.0 %collective-permute-start.20 = (f32[8,1,64]{2,1,0:T(1,128)S(1)}, f32[8,1,64]{2,1,0:T(1,128)S(1)}, u32[]{:S(2)}, u32[]{:S(2)}) collective-permute-start(f32[8,1,64]{2,1,0:T(1,128)S(1)} %get-tuple-element.65), channel_id=1, source_target_pairs={{64,0},{128,64},{192,128},{65,1},{129,65},{193,129},{66,2},{130,66... | collective-permute-start | bytes 6152 | tf_op jit(solution)/shard_map/ppermute | solution.py:20
  259.1 12.5 %collective-permute-start.24 = (f32[16,64,1]{2,1,0:T(8,128)S(1)}, f32[16,64,1]{2,1,0:T(8,128)S(1)}, u32[]{:S(2)}, u32[]{:S(2)}) collective-permute-start(f32[16,64,1]{2,1,0:T(8,128)S(1)} %get-tuple-element.51), channel_id=1, source_target_pairs={{0,16},{16,32},{32,48},{1,17},{17,33},{33,49},{2,18},{18,34},{34,5... | collective-permute-start | bytes 12296 | tf_op jit(solution)/shard_map/ppermute | solution.py:19
  260.5 15.0 %collective-permute-start.27 = (f32[16,64,1]{2,1,0:T(8,128)S(1)}, f32[16,64,1]{2,1,0:T(8,128)S(1)}, u32[]{:S(2)}, u32[]{:S(2)}) collective-permute-start(f32[16,64,1]{2,1,0:T(8,128)S(1)} %get-tuple-element.50), channel_id=1, source_target_pairs={{16,0},{32,16},{48,32},{17,1},{33,17},{49,33},{18,2},{34,18},{50,3... | collective-permute-start | bytes 12296 | tf_op jit(solution)/shard_map/ppermute | solution.py:20
  261.8 14.5 %collective-permute-start.28 = (f32[1,64,128]{2,1,0:T(8,128)S(1)}, f32[1,64,128]{2,1,0:T(8,128)S(1)}, u32[]{:S(2)}, u32[]{:S(2)}) collective-permute-start(f32[1,64,128]{2,1,0:T(8,128)S(1)} %get-tuple-element.48), channel_id=1, source_target_pairs={{1,0},{2,1},{3,2},{4,3},{5,4},{6,5},{7,6},{8,7},{9,8},{10,9},{11,1... | collective-permute-start | bytes 98312 | tf_op jit(solution)/shard_map/ppermute | solution.py:20
  264.1 12.2 %collective-permute-start.29 = (f32[1,64,128]{2,1,0:T(8,128)S(1)}, f32[1,64,128]{2,1,0:T(8,128)S(1)}, u32[]{:S(2)}, u32[]{:S(2)}) collective-permute-start(f32[1,64,128]{2,1,0:T(8,128)S(1)} %get-tuple-element.49), channel_id=1, source_target_pairs={{0,1},{1,2},{2,3},{3,4},{4,5},{5,6},{6,7},{7,8},{8,9},{9,10},{10,1... | collective-permute-start | bytes 98312 | tf_op jit(solution)/shard_map/ppermute | solution.py:19
  267.4 8.2 %collective-permute-start.25 = (f32[16,1,128]{2,1,0:T(1,128)S(1)}, f32[16,1,128]{2,1,0:T(1,128)S(1)}, u32[]{:S(2)}, u32[]{:S(2)}) collective-permute-start(f32[16,1,128]{2,1,0:T(1,128)S(1)} %get-tuple-element.52), channel_id=1, source_target_pairs={{0,64},{64,128},{128,192},{1,65},{65,129},{129,193},{2,66},{66,130... | collective-permute-start | bytes 24584 | tf_op jit(solution)/shard_map/ppermute | solution.py:19
  277.4 14.0 %collective-permute-start.33 = (f32[16,64,1]{2,1,0:T(8,128)S(1)}, f32[16,64,1]{2,1,0:T(8,128)S(1)}, u32[]{:S(2)}, u32[]{:S(2)}) collective-permute-start(f32[16,64,1]{2,1,0:T(8,128)S(1)} %get-tuple-element.45), channel_id=1, source_target_pairs={{16,0},{32,16},{48,32},{17,1},{33,17},{49,33},{18,2},{34,18},{50,3... | collective-permute-start | bytes 12296 | tf_op jit(solution)/shard_map/ppermute | solution.py:20
  278.7 13.6 %collective-permute-start.30 = (f32[16,64,1]{2,1,0:T(8,128)S(1)}, f32[16,64,1]{2,1,0:T(8,128)S(1)}, u32[]{:S(2)}, u32[]{:S(2)}) collective-permute-start(f32[16,64,1]{2,1,0:T(8,128)S(1)} %get-tuple-element.44), channel_id=1, source_target_pairs={{0,16},{16,32},{32,48},{1,17},{17,33},{33,49},{2,18},{18,34},{34,5... | collective-permute-start | bytes 12296 | tf_op jit(solution)/shard_map/ppermute | solution.py:19
  283.1 10.5 %collective-permute-start.34 = (f32[1,64,128]{2,1,0:T(8,128)S(1)}, f32[1,64,128]{2,1,0:T(8,128)S(1)}, u32[]{:S(2)}, u32[]{:S(2)}) collective-permute-start(f32[1,64,128]{2,1,0:T(8,128)S(1)} %slice.462), channel_id=1, source_target_pairs={{1,0},{2,1},{3,2},{4,3},{5,4},{6,5},{7,6},{8,7},{9,8},{10,9},{11,1... | collective-permute-start | bytes 98312 | tf_op jit(solution)/shard_map/ppermute | solution.py:20
  (13 other events, 93.4 us)
where the time goes:
time: 301 us; the launch traced here: 298 us
  local copies, waits for them, and re-layouts  96.4 us (32%)
  starting transfers between devices  92.5 us (31%)
  blocking collectives  45.2 us (15%)
  other arithmetic  31.7 us (11%)
  waiting for transfers between devices  24.9 us (8%)
  between operations  7.32 us (2%)
    ppermute x17, starting transfers between devices, extended(): lax.ppermute(last, axis, up)  62.3 us
    psum x4, blocking collectives, by_axis(): shard = lax.psum(shard, axis)  45.2 us
    reshape x1, local copies, waits for them, and re-layouts, local(): node_res.reshape(sx // 2, 2, sy // 2, 2, sz // 2, 2).sum(axis=(1, 3, 5))  34.9 us
    ppermute x18, starting transfers between devices, extended(): lax.ppermute(leading, axis, [(b, a) for a, b in up])  30.2 us
    reshape x1, local copies, waits for them, and re-layouts, local(): spread = jnp.broadcast_to(coarse_sol[:, None, :, None, :, None], (sx // 2...  24.4 us
    ppermute x18, waiting for transfers between devices, extended(): lax.ppermute(leading, axis, [(b, a) for a, b in up])  21.1 us
    reduce_sum x1, other arithmetic, local(): node_res.reshape(sx // 2, 2, sy // 2, 2, sz // 2, 2).sum(axis=(1, 3, 5))  12.2 us
    broadcast_in_dim x1, local copies, waits for them, and re-layouts, local(): jnp.broadcast_to(coarse_sol[:, None, :, None, :, None], (sx // 2, 2, sy /...  11.4 us
  transfers between devices with their start and end apart: 35, of which 9 were waited for; matrix products, arithmetic and copies ran while one was open for 6% of the time, Pallas kernels for 0%

commit v1 on v0

v1 whole, which is shorter than its diff:
```python
import functools

import jax
import jax.numpy as jnp
from jax import lax
from jax.experimental import pallas as pl
from jax.experimental.pallas import tpu as pltpu
from jax.sharding import PartitionSpec as P

MESH = pl.DeviceIdType.MESH
AXES = ("gx", "gy", "gz")
L = 128
F32 = jnp.float32


def iota(shape, dim):
    return lax.broadcasted_iota(jnp.int32, shape, dim)


class Message:
    def __init__(self, copy, sends, receives):
        self.copy, self.sends, self.receives = copy, sends, receives

    def start(self):
        pl.when(self.sends)(lambda: self.copy.start())

    def wait_recv(self):
        pl.when(self.receives)(lambda: self.copy.wait_recv())

    def wait_send(self):
        pl.when(self.sends)(lambda: self.copy.wait_send())


def kernel(
    sizes, res_h, ed_h, ns_h, cs_h, out_h,
    res, ed, ns, cs, sc, fg, tmp, cr, cd, v1, v2, wy1, wy2, a1s, ab, ff,
    rt_sc, rt_fg, rt_v1, rt_v2, rt_ab,
    xs_sc, xr_sc, xs_fg, xr_fg, xs_v1, xr_v1, xs_v2, xr_v2, xs_ab, xr_ab,
    ys_sc, yr_sc, ys_fg, yr_fg, ys_v1, yr_v1, ys_v2, yr_v2, ys_ab, yr_ab,
    ar1, ar2, in_sem, out_sem, send_sem, recv_sem, ar_send, ar_recv,
):
    _, Z, X, _ = res.shape
    ZC, XC = Z // 2, X // 2
    NB = Z // 2
    PC = L // XC
    NBC = ZC // PC
    me = {a: lax.axis_index(a) for a in AXES}
    used = []

    def message(src, dst, axis, step):
        i = len(used)
        last = sizes[axis] - 1
        copy = pltpu.make_async_remote_copy(
            src_ref=src, dst_ref=dst, send_sem=send_sem.at[i], recv_sem=recv_sem.at[i],
            device_id={axis: me[axis] + step}, device_id_type=MESH,
        )
        low, high = me[axis] > 0, me[axis] < last
        made = Message(copy, *((high, low) if step > 0 else (low, high)))
        used.append(made)
        return made

    def load(k):
        return (
            pltpu.make_async_copy(ed_h.at[k], ed.at[k], in_sem.at[2 * k]),
            pltpu.make_async_copy(res_h.at[k], res.at[k], in_sem.at[2 * k + 1]),
        )

    loads = [load(k) for k in range(3)]
    load_ns = pltpu.make_async_copy(ns_h, ns, in_sem.at[6])
    load_cs = pltpu.make_async_copy(cs_h, cs, in_sem.at[7])
    for k in (2, 1, 0):
        for copy in loads[k]:
            copy.start()
    load_ns.start()
    load_cs.start()

    zero_plane = jnp.zeros((X, L), F32)
    zero_coarse = jnp.zeros((XC, L), F32)
    for k in range(3):
        for z in (0, Z + 1):
            sc[k, z, 8 : 8 + X, :] = zero_plane
        ab[k, Z, 0:X, :] = zero_plane
    for z in (0, Z + 1):
        fg[z, 8 : 8 + X, :] = zero_plane
    for z in (0, ZC + 1):
        v1[z, 8 : 8 + XC, :] = zero_coarse
        v2[z, 8 : 8 + XC, :] = zero_coarse
    for ref in (xr_sc, xr_fg, xr_v1, xr_v2, xr_ab, yr_sc, yr_fg, yr_v1, yr_v2, yr_ab):
        ref[...] = jnp.zeros(ref.shape, F32)

    partners = [{"gz": lax.rem(me["gz"] + d, sizes["gz"])} for d in range(1, sizes["gz"])]
    plane = [
        {"gx": lax.rem(me["gx"] + dx, sizes["gx"]), "gy": lax.rem(me["gy"] + dy, sizes["gy"])}
        for dx in range(sizes["gx"]) for dy in range(sizes["gy"]) if dx or dy
    ]
    barrier = pltpu.get_barrier_semaphore()
    for other in partners + plane:
        pl.semaphore_signal(barrier, inc=1, device_id=other, device_id_type=MESH)

    lane = iota((X, L), 1)
    lane2 = iota((L, L), 1)
    lanec = iota((XC, L), 1)
    evenc = lanec % 2 == 0

    def put(packed, block, q):
        return jnp.where(lax.shift_right_logical(lane2, 1) == q, pltpu.roll(block, 2 * q + 1, 1), packed)

    def halo(rt, row, rows, q):
        return pltpu.roll(rt[row : row + rows, :], L - 1 - 2 * q, 1)

    def before(x, h, at):
        return jnp.where(at == 0, h, pltpu.roll(x, 1, 1))

    def after(x, h, at):
        return jnp.where(at == L - 1, h, pltpu.roll(x, L - 1, 1))

    def unpack(rt, got):
        n = got.shape[1]
        mixed = jnp.where(
            iota((n, L), 0) % 2 == 1, pltpu.roll(got[0], 1, 0), pltpu.roll(got[1], n - 1, 0)
        )
        rt[...] = jnp.concatenate([mixed, jnp.zeros((L - n, L), F32)], axis=0).T

    def scale(k, packed):
        for copy in loads[k]:
            copy.wait()

        def body(b, packed):
            block = []
            for p in range(2):
                z = 2 * b + p
                r = 1.0 / ed[k, z]
                ed[k, z] = r
                s = res[k, z] * r
                sc[k, z + 1, 8 : 8 + X, :] = s
                xs_sc[0, k, pl.ds(z, 1), :] = s[0:1]
                xs_sc[1, k, pl.ds(z, 1), :] = s[X - 1 : X]
                block.append(s)
            return put(packed, jnp.concatenate(block, axis=0), k * NB + b)

        return lax.fori_loop(0, NB, body, packed)

    packed = jnp.zeros((L, L), F32)
    for k in (2, 1, 0):
        packed = scale(k, packed)
    ys_sc[...] = packed.T[: 6 * NB]
    pl.semaphore_wait(barrier, len(partners) + len(plane))

    inner = pl.ds(8, X)
    sc_zu0 = message(sc.at[0, Z, inner, :], sc.at[0, 0, inner, :], "gz", 1)
    sc_zu = message(sc.at[1:3, Z, inner, :], sc.at[1:3, 0, inner, :], "gz", 1)
    sc_zd = message(sc.at[:, 1, inner, :], sc.at[:, Z + 1, inner, :], "gz", -1)
    sc_xu = message(xs_sc.at[1], xr_sc.at[0], "gx", 1)
    sc_xd = message(xs_sc.at[0], xr_sc.at[1], "gx", -1)
    sc_yu = message(ys_sc, yr_sc.at[0], "gy", 1)
    sc_yd = message(ys_sc, yr_sc.at[1], "gy", -1)
    for m in (sc_zu0, sc_xu, sc_yu, sc_yd, sc_xd, sc_zd, sc_zu):
        m.start()

    load_ns.wait()
    load_cs.wait()

    def invert(z, _):
        ns[z] = 1.0 / (6.0 + ns[z])
        return 0

    lax.fori_loop(0, Z, invert, 0)
    twice = (iota((L // 2, L), 0) == iota((L // 2, L), 1) // 2).astype(F32)
    wide = jnp.dot(
        cs[...].reshape(ZC * XC, L // 2), twice,
        precision=lax.Precision.HIGHEST, preferred_element_type=F32,
    )
    cd[...] = (1.0 / (6.0 + wide)).reshape(ZC, XC, L)

    for m in (sc_zu0, sc_xu, sc_yu, sc_yd, sc_xd):
        m.wait_recv()
    for k in range(3):
        sc[k, 1 : Z + 1, 7, :] = xr_sc[0, k]
        sc[k, 1 : Z + 1, 8 + X, :] = xr_sc[1, k]
    unpack(rt_sc, yr_sc)

    def guess(b, packed):
        block = []
        for p in range(2):
            z = 2 * b + p
            s0, s0m = sc[0, z + 1, 8 : 8 + X, :], sc[0, z, 8 : 8 + X, :]
            s1, s1m = sc[1, z + 1, 8 : 8 + X, :], sc[1, z + 1, 7 : 7 + X, :]
            s2 = sc[2, z + 1, 8 : 8 + X, :]
            s2m = before(s2, halo(rt_sc, p * X, X, 2 * NB + b), lane)
            g = ((s0m - s0) + (s1m - s1) + (s2m - s2)) * ns[z]
            fg[z + 1, 8 : 8 + X, :] = g
            xs_fg[0, pl.ds(z, 1), :] = g[0:1]
            xs_fg[1, pl.ds(z, 1), :] = g[X - 1 : X]
            block.append(g)
        return put(packed, jnp.concatenate(block, axis=0), b)

    packed = lax.fori_loop(0, NB, guess, jnp.zeros((L, L), F32))
    ys_fg[...] = packed.T[: 2 * NB]
    fg_m = [
        message(ys_fg, yr_fg.at[0], "gy", 1),
        message(ys_fg, yr_fg.at[1], "gy", -1),
        message(xs_fg.at[1], xr_fg.at[0], "gx", 1),
        message(xs_fg.at[0], xr_fg.at[1], "gx", -1),
        message(fg.at[Z, inner, :], fg.at[0, inner, :], "gz", 1),
        message(fg.at[1, inner, :], fg.at[Z + 1, inner, :], "gz", -1),
    ]
    for m in fg_m:
        m.start()

    def smooth(k):
        def body(b, _):
            for p in range(2):
                z = 2 * b + p
                s = sc[k, z + 1, 8 : 8 + X, :]
                h = halo(rt_sc, p * X, X, k * NB + b)
                n = sc[k, z, 8 : 8 + X, :] + sc[k, z + 2, 8 : 8 + X, :]
                n += sc[k, z + 1, 7 : 7 + X, :] + sc[k, z + 1, 9 : 9 + X, :]
                n += before(s, h, lane) + after(s, h, lane)
                res[k, z] = s + n * ed[k, z]
            return 0

        lax.fori_loop(0, NB, body, 0)

    sc_zu.wait_recv()
    sc_zd.wait_recv()
    smooth(0)

    for m in fg_m:
        m.wait_recv()
    fg[1 : Z + 1, 7, :] = xr_fg[0]
    fg[1 : Z + 1, 8 + X, :] = xr_fg[1]
    unpack(rt_fg, yr_fg)

    def swap(x):
        return jnp.where(evenc, pltpu.roll(x, L - 1, 1), pltpu.roll(x, 1, 1))

    def restrict(b, _):
        total = None
        for p in range(2):
            z = 2 * b + p
            g = fg[z + 1, 8 : 8 + X, :]
            h = halo(rt_fg, p * X, X, b)
            n = fg[z, 8 : 8 + X, :] + fg[z + 2, 8 : 8 + X, :]
            n += fg[z + 1, 7 : 7 + X, :] + fg[z + 1, 9 : 9 + X, :]
            n += before(g, h, lane) + after(g, h, lane)
            ab[0, z, 0:X, :] = g + n * ns[z]
            total = n if p == 0 else total + n
        tmp[b] = total
        u = tmp[b, pl.ds(0, XC, 2), :] + tmp[b, pl.ds(1, XC, 2), :]
        u = u + swap(u)
        cr[b] = u
        v = u * cd[b]
        v1[b + 1, 8 : 8 + XC, :] = v
        xs_v1[0, pl.ds(b, 1), :] = v[0:1]
        xs_v1[1, pl.ds(b, 1), :] = v[XC - 1 : XC]
        return 0

    lax.fori_loop(0, ZC, restrict, 0)

    def coarse_exchange(v, xs, xr, ys, yr):
        packed = jnp.zeros((L, L), F32)
        for q in range(NBC):
            packed = put(packed, v[1 + PC * q : 1 + PC * (q + 1), 8 : 8 + XC, :].reshape(L, L), q)
        ys[...] = packed.T[:8]
        mid = pl.ds(8, XC)
        sent = [
            message(ys, yr.at[0], "gy", 1),
            message(ys, yr.at[1], "gy", -1),
            message(xs.at[1], xr.at[0], "gx", 1),
            message(xs.at[0], xr.at[1], "gx", -1),
            message(v.at[ZC, mid, :], v.at[0, mid, :], "gz", 1),
            message(v.at[1, mid, :], v.at[ZC + 1, mid, :], "gz", -1),
        ]
        for m in sent:
            m.start()
        return sent

    def coarse_arrive(sent, v, xr, yr, rt):
        for m in sent:
            m.wait_recv()
        v[1 : ZC + 1, 7, :] = xr[0]
        v[1 : ZC + 1, 8 + XC, :] = xr[1]
        unpack(rt, yr)

    def around(v, wy, rt, b):
        c = v[b + 1, 8 : 8 + XC, :]
        h = pltpu.roll(rt[pl.ds(pl.multiple_of((b % PC) * XC, XC), XC), :], L - 1 - 2 * (b // PC), 1)
        w = jnp.where(evenc, before(c, h, lanec), after(c, h, lanec))
        wy[b] = w
        n = v[b, 8 : 8 + XC, :] + v[b + 2, 8 : 8 + XC, :]
        n += v[b + 1, 7 : 7 + XC, :] + v[b + 1, 9 : 9 + XC, :]
        return c, n + (w + swap(w))

    v1_m = coarse_exchange(v1, xs_v1, xr_v1, ys_v1, yr_v1)
    smooth(1)
    coarse_arrive(v1_m, v1, xr_v1, yr_v1, rt_v1)

    def first(b, sums):
        g1, g2, h11, h12 = sums
        c, n = around(v1, wy1, rt_v1, b)
        r = cr[b]
        a = r - n
        a1s[b] = a
        w = a * cd[b]
        v2[b + 1, 8 : 8 + XC, :] = w
        xs_v2[0, pl.ds(b, 1), :] = w[0:1]
        xs_v2[1, pl.ds(b, 1), :] = w[XC - 1 : XC]
        return g1 + c * r, g2 + w * r, h11 + c * a, h12 + w * a

    sums = lax.fori_loop(0, ZC, first, (zero_coarse,) * 4)
    v2_m = coarse_exchange(v2, xs_v2, xr_v2, ys_v2, yr_v2)
    smooth(2)
    coarse_arrive(v2_m, v2, xr_v2, yr_v2, rt_v2)

    def second(b, h22):
        c, n = around(v2, wy2, rt_v2, b)
        return h22 + c * (a1s[b] - n)

    sums += (lax.fori_loop(0, ZC, second, zero_coarse),)

    row = jnp.zeros((1, L), F32)
    for i, s in enumerate(sums):
        one = jnp.sum(jnp.sum(s, axis=0, keepdims=True), axis=1, keepdims=True)
        row = jnp.where(iota((1, L), 1) == i, one, row)
    ar1[0] = row

    def spread_round(buf, others, base):
        copies = [
            pltpu.make_async_remote_copy(
                src_ref=buf.at[0], dst_ref=buf.at[d + 1], send_sem=ar_send.at[base + d],
                recv_sem=ar_recv.at[base + d], device_id=other, device_id_type=MESH,
            )
            for d, other in enumerate(others)
        ]
        for copy in copies:
            copy.start()
        return copies

    round1 = spread_round(ar1, partners, 0)

    def prolong(v, wy, j):
        def body(b, _):
            w = 3.0 * v[b + 1, 8 : 8 + XC, :] + wy[b]
            for px in range(2):
                wx = w + v[b + 1, 7 + 2 * px : 7 + 2 * px + XC, :]
                for pz in range(2):
                    z = 2 * b + pz
                    n = wx + v[b + 2 * pz, 8 : 8 + XC, :]
                    ab[j, z, pl.ds(px, XC, 2), :] = n * ns[z, pl.ds(px, XC, 2), :]
            return 0

        lax.fori_loop(0, ZC, body, 0)

    prolong(v1, wy1, 1)
    prolong(v2, wy2, 2)

    def fill(j):
        def body(b, packed):
            block = []
            for p in range(2):
                z = 2 * b + p
                x = ab[j, z, 0:X, :]
                xs_ab[j, pl.ds(z, 1), :] = x[0:1]
                block.append(x)
            return put(packed, jnp.concatenate(block, axis=0), j * NB + b)

        return body

    packed = jnp.zeros((L, L), F32)
    for j in range(3):
        packed = lax.fori_loop(0, NB, fill(j), packed)
    ys_ab[...] = packed.T[: 6 * NB]
    ab_m = [
        message(ab.at[:, 0, pl.ds(0, X), :], ab.at[:, Z, pl.ds(0, X), :], "gz", -1),
        message(xs_ab, xr_ab, "gx", -1),
        message(ys_ab, yr_ab, "gy", -1),
    ]
    for m in ab_m:
        m.start()

    for copy in round1:
        copy.wait_recv()
    ar2[0] = jnp.sum(ar1[...], axis=0)
    round2 = spread_round(ar2, plane, len(partners))

    for m in ab_m:
        m.wait_recv()
    ab[:, 0:Z, X, :] = xr_ab[...]
    rt_ab[...] = jnp.concatenate(
        [pltpu.roll(yr_ab[...], 6 * NB - 1, 0), jnp.zeros((L - 6 * NB, L), F32)], axis=0
    ).T

    for copy in round2:
        copy.wait_recv()
    total = jnp.sum(ar2[...], axis=0)
    g1, g2, h11, h12, h22 = (
        jnp.sum(jnp.where(iota((1, L), 1) == i, total, 0.0), axis=1, keepdims=True) for i in range(5)
    )
    c2 = (g2 - h12 * g1 / h11) / (h22 - h12 * h12 / h11)
    c1 = (g1 - h12 * c2) / h11

    def combine(z, _):
        ff[z, 0:X, :] = ab[0, z, 0:X, :] + c1 * ab[1, z, 0:X, :] + c2 * ab[2, z, 0:X, :]
        return 0

    lax.fori_loop(0, Z + 1, combine, 0)
    ff[0:Z, X, :] = ab[0, 0:Z, X, :] + c1 * ab[1, 0:Z, X, :] + c2 * ab[2, 0:Z, X, :]
    rt = rt_ab[...]
    rt_ab[...] = rt + c1 * pltpu.roll(rt, L - 2 * NB, 1) + c2 * pltpu.roll(rt, L - 4 * NB, 1)

    def store(b):
        part = pl.ds(2 * b, 2)
        return pltpu.make_async_copy(res.at[:, part], out_h.at[:, part], out_sem.at[b])

    def finish(b, _):
        for p in range(2):
            z = 2 * b + p
            f = ff[z, 0:X, :]
            h = halo(rt_ab, p * X, X, b)
            res[0, z] = res[0, z] + (ff[z + 1, 0:X, :] - f)
            res[1, z] = res[1, z] + (ff[z, 1 : X + 1, :] - f)
            res[2, z] = res[2, z] + (after(f, h, lane) - f)
        store(b).start()
        return 0

    lax.fori_loop(0, NB, finish, 0)

    for m in used:
        m.wait_send()
    for copy in round1 + round2:
        copy.wait_send()
    for b in range(NB):
        store(b).wait()


def solution(mesh):
    sizes = dict(mesh.shape)
    n_ar = sizes["gz"] - 1 + sizes["gx"] * sizes["gy"] - 1

    def local(residual, edge_diag, node_shift, coarse_shift):
        _, Z, X, Y = residual.shape
        ZC, XC, NB = Z // 2, X // 2, Z // 2
        assert X == 64 and Y == L and Z % 8 == 0

        def v(*shape):
            return pltpu.VMEM(shape, F32)

        scratch = [
            v(3, Z, X, L), v(3, Z, X, L), v(Z, X, L), v(ZC, XC, L // 2),
            v(3, Z + 2, X + 16, L), v(Z + 2, X + 16, L), v(ZC, X, L),
            v(ZC, XC, L), v(ZC, XC, L),
            v(ZC + 2, XC + 16, L), v(ZC + 2, XC + 16, L),
            v(ZC, XC, L), v(ZC, XC, L), v(ZC, XC, L),
            v(3, Z + 1, X + 8, L), v(Z + 1, X + 8, L),
            v(L, L), v(L, L), v(L, L), v(L, L), v(L, L),
            v(2, 3, Z, L), v(2, 3, Z, L), v(2, Z, L), v(2, Z, L),
            v(2, ZC, L), v(2, ZC, L), v(2, ZC, L), v(2, ZC, L), v(3, Z, L), v(3, Z, L),
            v(6 * NB, L), v(2, 6 * NB, L), v(2 * NB, L), v(2, 2 * NB, L),
            v(8, L), v(2, 8, L), v(8, L), v(2, 8, L), v(6 * NB, L), v(6 * NB, L),
            v(sizes["gz"], 1, L), v(sizes["gx"] * sizes["gy"], 1, L),
            pltpu.SemaphoreType.DMA((8,)), pltpu.SemaphoreType.DMA((NB,)),
            pltpu.SemaphoreType.DMA((32,)), pltpu.SemaphoreType.DMA((32,)),
            pltpu.SemaphoreType.DMA((n_ar,)), pltpu.SemaphoreType.DMA((n_ar,)),
        ]
        return pl.pallas_call(
            functools.partial(kernel, sizes),
            out_shape=jax.ShapeDtypeStruct(residual.shape, F32),
            in_specs=[pl.BlockSpec(memory_space=pl.ANY)] * 4,
            out_specs=pl.BlockSpec(memory_space=pl.ANY),
            scratch_shapes=scratch,
            compiler_params=pltpu.CompilerParams(
                collective_id=0, has_side_effects=True, vmem_limit_bytes=48 * 1024 * 1024
            ),
        )(residual, edge_diag, node_shift, coarse_shift)

    fine, coarse = P(None, "gz", "gx", "gy"), P("gz", "gx", "gy")
    return jax.shard_map(
        local, mesh=mesh, in_specs=(fine, fine, coarse, coarse), out_specs=fine, check_vma=False
    )
```

time: 301 us -> 47.1 us (0.16)
  starting transfers between devices: 92.5 us -> 0 us
  local copies, waits for them, and re-layouts: 96.4 us -> 5.9 us
  blocking collectives: 45.2 us -> 0 us
  Pallas kernels: 0 us -> 41 us
  other arithmetic: 31.7 us -> 0 us
  waiting for transfers between devices: 24.9 us -> 0 us
  between operations: 7.32 us -> 0.01 us
    ppermute x35 -> x0, starting transfers between devices: 92.5 us -> none  [the longest x17 62.3 us: extended(): lax.ppermute(last, axis, up)]
    reshape x2 -> x0, local copies, waits for them, and re-layouts: 59.3 us -> none  [the longest x1 34.9 us: local(): node_res.reshape(sx // 2, 2, sy // 2, 2, sz // 2, 2).sum(axis=(1, 3, 5))]
    psum x4 -> x0, blocking collectives: 45.2 us -> none  [by_axis(): shard = lax.psum(shard, axis)]
    pallas_call x0 -> x1, Pallas kernels: none -> 41 us  [local(): pl.pallas_call(functools.partial(kernel, sizes), out_shape=jax.ShapeDtype...]
    ppermute x35 -> x0, waiting for transfers between devices: 24.9 us -> none  [the longest x18 21.1 us: extended(): lax.ppermute(leading, axis, [(b, a) for a, b in up])]
    reduce_sum x3 -> x0, other arithmetic: 14.2 us -> none  [the longest x1 12.2 us: local(): node_res.reshape(sx // 2, 2, sy // 2, 2, sz // 2, 2).sum(axis=(1, 3, 5))]
    slice x20 -> x0, local copies, waits for them, and re-layouts: 12.2 us -> none  [the longest x10 8.47 us: extended(): last = lax.slice_in_dim(shard, length - width, length, axis=dim)]
    broadcast_in_dim x1 -> x0, local copies, waits for them, and re-layouts: 11.4 us -> none  [local(): jnp.broadcast_to(coarse_sol[:, None, :, None, :, None], (sx // 2, 2, sy /...]
  transfers between devices with their start and end apart: 35 -> 0, of which waited for: 9 -> 0; matrix products, arithmetic and copies ran while one was open for 6% -> 0% of each run, Pallas kernels for 0% -> 0%
where the time goes in v1:
time: 47.1 us; the launch traced here: 46.9 us
  Pallas kernels  41 us (87%)
  local copies, waits for them, and re-layouts  5.9 us (13%)
    pallas_call x1, Pallas kernels, local(): pl.pallas_call(functools.partial(kernel, sizes), out_shape=jax.ShapeDtype...  41 us
    unnamed x9, local copies, waits for them, and re-layouts  5.9 us

profile of v1, /device:TPU:1, one launch (start us, length us, event | category | flops | bytes accessed | tf_op | source)
XLA Modules:
  0.0 46.9 jit_solution(760242126684346377)
XLA Ops:
  0.0 0.0 copy-start
  0.0 1.4 %copy-done = f32[3,16,64,128]{3,2,1,0:T(8,128)S(1)} copy-done((f32[3,16,64,128]{3,2,1,0:T(8,128)S(1)}, f32[3,16,64,128]{3,2,1,0:T(8,128)}, u32[]{:S(2)}) %copy-start) | copy-done | bytes 1572888
  1.4 0.0 copy-start.1
  1.4 1.4 %copy-done.1 = f32[3,16,64,128]{3,2,1,0:T(8,128)S(1)} copy-done((f32[3,16,64,128]{3,2,1,0:T(8,128)S(1)}, f32[3,16,64,128]{3,2,1,0:T(8,128)}, u32[]{:S(2)}) %copy-start.1) | copy-done | bytes 1572888
  2.8 0.0 copy-start.2
  2.8 1.0 %copy-done.2 = f32[16,64,128]{2,1,0:T(8,128)S(1)} copy-done((f32[16,64,128]{2,1,0:T(8,128)S(1)}, f32[16,64,128]{2,1,0:T(8,128)}, u32[]{:S(2)}) %copy-start.2) | copy-done | bytes 524312
  3.9 0.0 copy-start.3
  3.9 0.9 %copy-done.3 = f32[8,32,64]{2,1,0:T(8,128)S(1)} copy-done((f32[8,32,64]{2,1,0:T(8,128)S(1)}, f32[8,32,64]{2,1,0:T(8,128)}, u32[]{:S(2)}) %copy-start.3) | copy-done | bytes 65560
  4.8 41.0 %shard_map.46 = f32[3,16,64,128]{3,2,1,0:T(8,128)S(1)} custom-call(f32[3,16,64,128]{3,2,1,0:T(8,128)S(1)} %copy-done, f32[3,16,64,128]{3,2,1,0:T(8,128)S(1)} %copy-done.1, f32[16,64,128]{2,1,0:T(8,128)S(1)} %copy-done.2, f32[8,32,64]{2,1,0:T(8,128)S(1)} %copy-done.3), custom_call_target="tpu_custom_call" | custom-call | tf_op jit(solution)/shard_map/pallas_call | solution.py:465
  45.7 1.1 %copy.6 = f32[3,16,64,128]{3,2,1,0:T(8,128)} copy(f32[3,16,64,128]{3,2,1,0:T(8,128)S(1)} %shard_map.46) | data formatting | bytes 3145728
Async XLA Ops:
  0.0 1.4 %copy-start = (f32[3,16,64,128]{3,2,1,0:T(8,128)S(1)}, f32[3,16,64,128]{3,2,1,0:T(8,128)}, u32[]{:S(2)}) copy-start(f32[3,16,64,128]{3,2,1,0:T(8,128)} %res_h.1) | copy-start | bytes 4718596
  1.4 1.4 %copy-start.1 = (f32[3,16,64,128]{3,2,1,0:T(8,128)S(1)}, f32[3,16,64,128]{3,2,1,0:T(8,128)}, u32[]{:S(2)}) copy-start(f32[3,16,64,128]{3,2,1,0:T(8,128)} %ed_h.1) | copy-start | bytes 4718596
  2.8 1.0 %copy-start.2 = (f32[16,64,128]{2,1,0:T(8,128)S(1)}, f32[16,64,128]{2,1,0:T(8,128)}, u32[]{:S(2)}) copy-start(f32[16,64,128]{2,1,0:T(8,128)} %ns_h.1) | copy-start | bytes 1572868
  3.9 0.9 %copy-start.3 = (f32[8,32,64]{2,1,0:T(8,128)S(1)}, f32[8,32,64]{2,1,0:T(8,128)}, u32[]{:S(2)}) copy-start(f32[8,32,64]{2,1,0:T(8,128)} %cs_h.1) | copy-start | bytes 196612

commit v2 on v1

v2 whole, which is shorter than its diff:
```python
import functools

import jax
import jax.numpy as jnp
from jax import lax
from jax.experimental import pallas as pl
from jax.experimental.pallas import tpu as pltpu
from jax.sharding import PartitionSpec as P

MESH = pl.DeviceIdType.MESH
AXES = ("gx", "gy", "gz")
L = 128
F32 = jnp.float32


def iota(shape, dim):
    return lax.broadcasted_iota(jnp.int32, shape, dim)


class Message:
    def __init__(self, copy, sends, receives):
        self.copy, self.sends, self.receives = copy, sends, receives

    def start(self):
        pl.when(self.sends)(lambda: self.copy.start())

    def wait_recv(self):
        pl.when(self.receives)(lambda: self.copy.wait_recv())

    def wait_send(self):
        pl.when(self.sends)(lambda: self.copy.wait_send())


def kernel(
    sizes, res_h, ed_h, ns_h, cs_h, out,
    res, ed, ns, cs, sc, fg, tmp, cr, cd, v1, v2, wy1, wy2, a1s, ab, face_e, face_r,
    rt_g, rt_sc, rt_fg, rt_v1, rt_v2, rt_ab,
    xs_sc, xr_sc, xs_fg, xr_fg, xs_v1, xr_v1, xs_v2, xr_v2, xs_ab, xr_ab,
    ys_sc, yr_sc, ys_fg, yr_fg, ys_v1, yr_v1, ys_v2, yr_v2, ys_ab, yr_ab,
    ar1, ar2, in_sem, send_sem, recv_sem, ar_send, ar_recv,
):
    _, Z, X, _ = res.shape
    ZC, XC = Z // 2, X // 2
    NB = Z // 2
    PC = L // XC
    NBC = ZC // PC
    me = {a: lax.axis_index(a) for a in AXES}
    used = []

    def message(src, dst, axis, step):
        i = len(used)
        last = sizes[axis] - 1
        copy = pltpu.make_async_remote_copy(
            src_ref=src, dst_ref=dst, send_sem=send_sem.at[i], recv_sem=recv_sem.at[i],
            device_id={axis: me[axis] + step}, device_id_type=MESH,
        )
        low, high = me[axis] > 0, me[axis] < last
        made = Message(copy, *((high, low) if step > 0 else (low, high)))
        used.append(made)
        return made

    def load(i, pick, into):
        return (
            pltpu.make_async_copy(pick(ed_h), into(ed, face_e), in_sem.at[2 * i]),
            pltpu.make_async_copy(pick(res_h), into(res, face_r), in_sem.at[2 * i + 1]),
        )

    loads = [
        load(0, lambda h: h.at[0, Z - 1], lambda v, f: v.at[0, Z - 1]),
        load(1, lambda h: h.at[1, :, pl.ds(X - 8, 8), :], lambda v, f: f),
        load(2, lambda h: h.at[2], lambda v, f: v.at[2]),
        load(3, lambda h: h.at[1], lambda v, f: v.at[1]),
        load(4, lambda h: h.at[0, pl.ds(0, Z - 1)], lambda v, f: v.at[0, pl.ds(0, Z - 1)]),
    ]
    load_ns = pltpu.make_async_copy(ns_h, ns, in_sem.at[10])
    load_cs = pltpu.make_async_copy(cs_h, cs, in_sem.at[11])
    for pair in loads:
        for copy in pair:
            copy.start()
    load_ns.start()
    load_cs.start()

    partners = [{"gz": lax.rem(me["gz"] + d, sizes["gz"])} for d in range(1, sizes["gz"])]
    plane = [
        {"gx": lax.rem(me["gx"] + dx, sizes["gx"]), "gy": lax.rem(me["gy"] + dy, sizes["gy"])}
        for dx in range(sizes["gx"]) for dy in range(sizes["gy"]) if dx or dy
    ]
    near = [partners[0], partners[-1], *(
        {"gx": lax.rem(me["gx"] + d, sizes["gx"])} for d in (1, sizes["gx"] - 1)
    ), *({"gy": lax.rem(me["gy"] + d, sizes["gy"])} for d in (1, sizes["gy"] - 1))]
    barrier = pltpu.get_barrier_semaphore()
    for other in partners + plane:
        pl.semaphore_signal(barrier, inc=1, device_id=other, device_id_type=MESH)

    zero_plane = jnp.zeros((X, L), F32)
    zero_coarse = jnp.zeros((XC, L), F32)
    for k in range(3):
        for z in (0, Z + 1):
            sc[k, z, 8 : 8 + X, :] = zero_plane
        ab[k, Z, 0:X, :] = zero_plane
    for z in (0, Z + 1):
        fg[z, 8 : 8 + X, :] = zero_plane
    for z in (0, ZC + 1):
        v1[z, 8 : 8 + XC, :] = zero_coarse
        v2[z, 8 : 8 + XC, :] = zero_coarse
    for ref in (xr_sc, xr_fg, xr_v1, xr_v2, xr_ab, yr_sc, yr_fg, yr_v1, yr_v2, yr_ab):
        ref[...] = jnp.zeros(ref.shape, F32)

    for other in near:
        pl.semaphore_signal(barrier, inc=1, device_id=other, device_id_type=MESH)

    lane = iota((X, L), 1)
    lane2 = iota((L, L), 1)
    lanec = iota((XC, L), 1)
    evenc = lanec % 2 == 0

    def put(packed, block, q):
        return jnp.where(lax.shift_right_logical(lane2, 1) == q, pltpu.roll(block, 2 * q + 1, 1), packed)

    def halo(rt, row, rows, q):
        return pltpu.roll(rt[pl.ds(row, rows), :], L - 1 - 2 * q, 1)

    def before(x, h, at):
        return jnp.where(at == 0, h, pltpu.roll(x, 1, 1))

    def after(x, h, at):
        return jnp.where(at == L - 1, h, pltpu.roll(x, L - 1, 1))

    def unpack(rt, low, high):
        n = low.shape[0]
        mixed = jnp.where(iota((n, L), 0) % 2 == 1, pltpu.roll(low, 1, 0), pltpu.roll(high, n - 1, 0))
        rt[...] = jnp.concatenate([mixed, jnp.zeros((L - n, L), F32)], axis=0).T

    def each(n, body, init):
        return lax.fori_loop(0, n, body, init, unroll=True)

    inner = pl.ds(8, X)
    third = 2 * NB
    sc_zu0 = message(sc.at[0, Z, inner, :], sc.at[0, 0, inner, :], "gz", 1)
    sc_xu1 = message(xs_sc.at[1, 1], xr_sc.at[0, 1], "gx", 1)
    sc_yu2 = message(ys_sc.at[pl.ds(2 * third, third)], yr_sc.at[0, pl.ds(2 * third, third)], "gy", 1)
    rest = [
        message(xs_sc.at[1, 0], xr_sc.at[0, 0], "gx", 1),
        message(xs_sc.at[1, 2], xr_sc.at[0, 2], "gx", 1),
        message(xs_sc.at[0], xr_sc.at[1], "gx", -1),
        message(ys_sc.at[pl.ds(0, 2 * third)], yr_sc.at[0, pl.ds(0, 2 * third)], "gy", 1),
        message(ys_sc, yr_sc.at[1], "gy", -1),
        message(sc.at[1:3, Z, inner, :], sc.at[1:3, 0, inner, :], "gz", 1),
        message(sc.at[:, 1, inner, :], sc.at[:, Z + 1, inner, :], "gz", -1),
    ]

    def arrived(i):
        for copy in loads[i]:
            copy.wait()

    def scale(k, z):
        r = 1.0 / ed[k, z]
        ed[k, z] = r
        s = res[k, z] * r
        sc[k, z + 1, 8 : 8 + X, :] = s
        xs_sc[0, k, pl.ds(z, 1), :] = s[0:1]
        if k != 1:
            xs_sc[1, k, pl.ds(z, 1), :] = s[X - 1 : X]
        return s

    def scale_all(k, packed, first):
        def body(b, packed):
            block = []
            for p in range(2):
                z = 2 * b + p
                block.append(scale(k, z))
            return put(packed, jnp.concatenate(block, axis=0), first + b)

        return each(NB, body, packed)

    arrived(0)
    scale(0, Z - 1)
    arrived(1)
    xs_sc[1, 1] = face_r[:, 7, :] * (1.0 / face_e[:, 7, :])
    arrived(2)
    ys_sc[2 * third :] = scale_all(2, jnp.zeros((L, L), F32), 0).T[:third]
    pl.semaphore_wait(barrier, len(partners) + len(plane) + len(near))
    for m in (sc_yu2, sc_xu1, sc_zu0):
        m.start()
    arrived(3)
    packed = scale_all(1, jnp.zeros((L, L), F32), NB)
    arrived(4)

    def bulk(b, packed):
        block = [scale(0, 2 * b), scale(0, 2 * b + 1)]
        return put(packed, jnp.concatenate(block, axis=0), b)

    packed = each(NB - 1, bulk, packed)
    block = [scale(0, Z - 2), sc[0, Z, 8 : 8 + X, :]]
    packed = put(packed, jnp.concatenate(block, axis=0), NB - 1)
    ys_sc[0 : 2 * third] = packed.T[: 2 * third]
    for m in rest:
        m.start()

    load_ns.wait()
    load_cs.wait()

    def invert(z, _):
        ns[z] = 1.0 / (6.0 + ns[z])
        return 0

    lax.fori_loop(0, Z, invert, 0, unroll=2)
    twice = (iota((L // 2, L), 0) == iota((L // 2, L), 1) // 2).astype(F32)
    wide = jnp.dot(
        cs[...].reshape(ZC * XC, L // 2), twice,
        precision=lax.Precision.HIGHEST, preferred_element_type=F32,
    )
    cd[...] = (1.0 / (6.0 + wide)).reshape(ZC, XC, L)

    for m in (sc_yu2, sc_xu1, sc_zu0):
        m.wait_recv()
    sc[1, 1 : Z + 1, 7, :] = xr_sc[0, 1]
    low = yr_sc[0, 2 * third :]
    unpack(rt_g, low, jnp.zeros_like(low))

    def guess(b, packed):
        block = []
        for p in range(2):
            z = 2 * b + p
            s0, s0m = sc[0, z + 1, 8 : 8 + X, :], sc[0, z, 8 : 8 + X, :]
            s1, s1m = sc[1, z + 1, 8 : 8 + X, :], sc[1, z + 1, 7 : 7 + X, :]
            s2 = sc[2, z + 1, 8 : 8 + X, :]
            s2m = before(s2, halo(rt_g, p * X, X, b), lane)
            g = ((s0m - s0) + (s1m - s1) + (s2m - s2)) * ns[z]
            fg[z + 1, 8 : 8 + X, :] = g
            xs_fg[0, pl.ds(z, 1), :] = g[0:1]
            xs_fg[1, pl.ds(z, 1), :] = g[X - 1 : X]
            block.append(g)
        return put(packed, jnp.concatenate(block, axis=0), b)

    packed = each(NB, guess, jnp.zeros((L, L), F32))
    ys_fg[...] = packed.T[: 2 * NB]
    fg_m = [
        message(ys_fg, yr_fg.at[0], "gy", 1),
        message(ys_fg, yr_fg.at[1], "gy", -1),
        message(xs_fg.at[1], xr_fg.at[0], "gx", 1),
        message(xs_fg.at[0], xr_fg.at[1], "gx", -1),
        message(fg.at[Z, inner, :], fg.at[0, inner, :], "gz", 1),
        message(fg.at[1, inner, :], fg.at[Z + 1, inner, :], "gz", -1),
    ]
    for m in fg_m:
        m.start()

    for m in fg_m:
        m.wait_recv()
    fg[1 : Z + 1, 7, :] = xr_fg[0]
    fg[1 : Z + 1, 8 + X, :] = xr_fg[1]
    unpack(rt_fg, yr_fg[0], yr_fg[1])

    def swap(x):
        return jnp.where(evenc, pltpu.roll(x, L - 1, 1), pltpu.roll(x, 1, 1))

    def restrict(b, _):
        total = None
        for p in range(2):
            z = 2 * b + p
            g = fg[z + 1, 8 : 8 + X, :]
            h = halo(rt_fg, p * X, X, b)
            n = fg[z, 8 : 8 + X, :] + fg[z + 2, 8 : 8 + X, :]
            n += fg[z + 1, 7 : 7 + X, :] + fg[z + 1, 9 : 9 + X, :]
            n += before(g, h, lane) + after(g, h, lane)
            ab[0, z, 0:X, :] = g + n * ns[z]
            total = n if p == 0 else total + n
        tmp[b] = total
        return 0

    each(ZC, restrict, 0)

    def direction(b, _):
        u = tmp[b, pl.ds(0, XC, 2), :] + tmp[b, pl.ds(1, XC, 2), :]
        u = u + swap(u)
        cr[b] = u
        v = u * cd[b]
        v1[b + 1, 8 : 8 + XC, :] = v
        xs_v1[0, pl.ds(b, 1), :] = v[0:1]
        xs_v1[1, pl.ds(b, 1), :] = v[XC - 1 : XC]
        return 0

    each(ZC, direction, 0)

    def coarse_exchange(v, xs, xr, ys, yr):
        packed = jnp.zeros((L, L), F32)
        for q in range(NBC):
            packed = put(packed, v[1 + PC * q : 1 + PC * (q + 1), 8 : 8 + XC, :].reshape(L, L), q)
        ys[...] = packed.T[:8]
        mid = pl.ds(8, XC)
        sent = [
            message(ys, yr.at[0], "gy", 1),
            message(ys, yr.at[1], "gy", -1),
            message(xs.at[1], xr.at[0], "gx", 1),
            message(xs.at[0], xr.at[1], "gx", -1),
            message(v.at[ZC, mid, :], v.at[0, mid, :], "gz", 1),
            message(v.at[1, mid, :], v.at[ZC + 1, mid, :], "gz", -1),
        ]
        for m in sent:
            m.start()
        return sent

    def coarse_arrive(sent, v, xr, yr, rt):
        for m in sent:
            m.wait_recv()
        v[1 : ZC + 1, 7, :] = xr[0]
        v[1 : ZC + 1, 8 + XC, :] = xr[1]
        unpack(rt, yr[0], yr[1])

    def around(v, wy, rt, b):
        c = v[b + 1, 8 : 8 + XC, :]
        h = halo(rt, (b % PC) * XC, XC, b // PC)
        w = jnp.where(evenc, before(c, h, lanec), after(c, h, lanec))
        wy[b] = w
        n = v[b, 8 : 8 + XC, :] + v[b + 2, 8 : 8 + XC, :]
        n += v[b + 1, 7 : 7 + XC, :] + v[b + 1, 9 : 9 + XC, :]
        return c, n + (w + swap(w))

    v1_m = coarse_exchange(v1, xs_v1, xr_v1, ys_v1, yr_v1)
    coarse_arrive(v1_m, v1, xr_v1, yr_v1, rt_v1)

    def first(b, sums):
        g1, g2, h11, h12 = sums
        c, n = around(v1, wy1, rt_v1, b)
        r = cr[b]
        a = r - n
        a1s[b] = a
        w = a * cd[b]
        v2[b + 1, 8 : 8 + XC, :] = w
        xs_v2[0, pl.ds(b, 1), :] = w[0:1]
        xs_v2[1, pl.ds(b, 1), :] = w[XC - 1 : XC]
        return g1 + c * r, g2 + w * r, h11 + c * a, h12 + w * a

    sums = each(ZC, first, (zero_coarse,) * 4)
    v2_m = coarse_exchange(v2, xs_v2, xr_v2, ys_v2, yr_v2)
    coarse_arrive(v2_m, v2, xr_v2, yr_v2, rt_v2)

    def second(b, h22):
        c, n = around(v2, wy2, rt_v2, b)
        return h22 + c * (a1s[b] - n)

    sums += (each(ZC, second, zero_coarse),)

    row = jnp.zeros((1, L), F32)
    for i, s in enumerate(sums):
        one = jnp.sum(jnp.sum(s, axis=0, keepdims=True), axis=1, keepdims=True)
        row = jnp.where(iota((1, L), 1) == i, one, row)
    ar1[0] = row

    def spread_round(buf, others, base):
        copies = [
            pltpu.make_async_remote_copy(
                src_ref=buf.at[0], dst_ref=buf.at[d + 1], send_sem=ar_send.at[base + d],
                recv_sem=ar_recv.at[base + d], device_id=other, device_id_type=MESH,
            )
            for d, other in enumerate(others)
        ]
        for copy in copies:
            copy.start()
        return copies

    round1 = spread_round(ar1, partners, 0)

    def prolong(v, wy, j):
        def body(b, _):
            w = 3.0 * v[b + 1, 8 : 8 + XC, :] + wy[b]
            for px in range(2):
                wx = w + v[b + 1, 7 + 2 * px : 7 + 2 * px + XC, :]
                for pz in range(2):
                    z = 2 * b + pz
                    n = wx + v[b + 2 * pz, 8 : 8 + XC, :]
                    ab[j, z, pl.ds(px, XC, 2), :] = n * ns[z, pl.ds(px, XC, 2), :]
            return 0

        each(ZC, body, 0)

    prolong(v1, wy1, 1)
    prolong(v2, wy2, 2)

    def fill(j):
        def body(b, packed):
            block = []
            for p in range(2):
                z = 2 * b + p
                x = ab[j, z, 0:X, :]
                xs_ab[j, pl.ds(z, 1), :] = x[0:1]
                block.append(x)
            return put(packed, jnp.concatenate(block, axis=0), j * NB + b)

        return body

    packed = jnp.zeros((L, L), F32)
    for j in range(3):
        packed = each(NB, fill(j), packed)
    ys_ab[...] = packed.T[: 6 * NB]
    ab_m = [
        message(ab.at[:, 0, pl.ds(0, X), :], ab.at[:, Z, pl.ds(0, X), :], "gz", -1),
        message(xs_ab, xr_ab, "gx", -1),
        message(ys_ab, yr_ab, "gy", -1),
    ]
    for m in ab_m:
        m.start()

    def smooth(k):
        def body(b, _):
            for p in range(2):
                z = 2 * b + p
                s = sc[k, z + 1, 8 : 8 + X, :]
                h = halo(rt_sc, p * X, X, k * NB + b)
                n = sc[k, z, 8 : 8 + X, :] + sc[k, z + 2, 8 : 8 + X, :]
                n += sc[k, z + 1, 7 : 7 + X, :] + sc[k, z + 1, 9 : 9 + X, :]
                n += before(s, h, lane) + after(s, h, lane)
                out[k, z] = s + n * ed[k, z]
            return 0

        each(NB, body, 0)

    def fill_rows():
        for m in rest:
            m.wait_recv()
        for k in range(3):
            if k != 1:
                sc[k, 1 : Z + 1, 7, :] = xr_sc[0, k]
            sc[k, 1 : Z + 1, 8 + X, :] = xr_sc[1, k]
        unpack(rt_sc, yr_sc[0], yr_sc[1])

    fill_rows()
    smooth(0)

    for copy in round1:
        copy.wait_recv()
    ar2[0] = jnp.sum(ar1[...], axis=0)
    round2 = spread_round(ar2, plane, len(partners))

    smooth(1)
    smooth(2)
    for m in ab_m:
        m.wait_recv()
    ab[:, 0:Z, X, :] = xr_ab[...]
    rt_ab[...] = jnp.concatenate(
        [pltpu.roll(yr_ab[...], 6 * NB - 1, 0), jnp.zeros((L - 6 * NB, L), F32)], axis=0
    ).T

    def gradient(j, into, add):
        def body(b, _):
            for p in range(2):
                z = 2 * b + p
                f = ab[j, z, 0:X, :]
                h = halo(rt_ab, p * X, X, j * NB + b)
                d = (ab[j, z + 1, 0:X, :] - f, ab[j, z, 1 : X + 1, :] - f, after(f, h, lane) - f)
                for k in range(3):
                    into[k, z] = into[k, z] + d[k] if add else d[k]
            return 0

        each(NB, body, 0)

    gradient(0, out, True)
    gradient(1, res, False)
    gradient(2, ed, False)

    for copy in round2:
        copy.wait_recv()
    total = jnp.sum(ar2[...], axis=0)
    g1, g2, h11, h12, h22 = (
        jnp.sum(jnp.where(iota((1, L), 1) == i, total, 0.0), axis=1, keepdims=True) for i in range(5)
    )
    c2 = (g2 - h12 * g1 / h11) / (h22 - h12 * h12 / h11)
    c1 = (g1 - h12 * c2) / h11

    def finish(z, _):
        for k in range(3):
            out[k, z] = out[k, z] + c1 * res[k, z] + c2 * ed[k, z]
        return 0

    lax.fori_loop(0, Z, finish, 0, unroll=2)

    for m in used:
        m.wait_send()
    for copy in round1 + round2:
        copy.wait_send()


def solution(mesh):
    sizes = dict(mesh.shape)
    n_ar = sizes["gz"] - 1 + sizes["gx"] * sizes["gy"] - 1

    def local(residual, edge_diag, node_shift, coarse_shift):
        _, Z, X, Y = residual.shape
        ZC, XC, NB = Z // 2, X // 2, Z // 2
        assert X == 64 and Y == L and Z % 8 == 0

        def v(*shape):
            return pltpu.VMEM(shape, F32)

        scratch = [
            v(3, Z, X, L), v(3, Z, X, L), v(Z, X, L), v(ZC, XC, L // 2),
            v(3, Z + 2, X + 16, L), v(Z + 2, X + 16, L), v(ZC, X, L),
            v(ZC, XC, L), v(ZC, XC, L),
            v(ZC + 2, XC + 16, L), v(ZC + 2, XC + 16, L),
            v(ZC, XC, L), v(ZC, XC, L), v(ZC, XC, L),
            v(3, Z + 1, X + 8, L), v(Z, 8, L), v(Z, 8, L),
            v(L, L), v(L, L), v(L, L), v(L, L), v(L, L), v(L, L),
            v(2, 3, Z, L), v(2, 3, Z, L), v(2, Z, L), v(2, Z, L),
            v(2, ZC, L), v(2, ZC, L), v(2, ZC, L), v(2, ZC, L), v(3, Z, L), v(3, Z, L),
            v(6 * NB, L), v(2, 6 * NB, L), v(2 * NB, L), v(2, 2 * NB, L),
            v(8, L), v(2, 8, L), v(8, L), v(2, 8, L), v(6 * NB, L), v(6 * NB, L),
            v(sizes["gz"], 1, L), v(sizes["gx"] * sizes["gy"], 1, L),
            pltpu.SemaphoreType.DMA((12,)),
            pltpu.SemaphoreType.DMA((32,)), pltpu.SemaphoreType.DMA((32,)),
            pltpu.SemaphoreType.DMA((n_ar,)), pltpu.SemaphoreType.DMA((n_ar,)),
        ]
        return pl.pallas_call(
            functools.partial(kernel, sizes),
            out_shape=jax.ShapeDtypeStruct(residual.shape, F32),
            in_specs=[pl.BlockSpec(memory_space=pl.ANY)] * 4,
            out_specs=pl.BlockSpec(memory_space=pltpu.VMEM),
            scratch_shapes=scratch,
            compiler_params=pltpu.CompilerParams(
                collective_id=0, has_side_effects=True, vmem_limit_bytes=48 * 1024 * 1024
            ),
        )(*(
            pltpu.with_memory_space_constraint(x, pltpu.HBM)
            for x in (residual, edge_diag, node_shift, coarse_shift)
        ))

    fine, coarse = P(None, "gz", "gx", "gy"), P("gz", "gx", "gy")
    return jax.shard_map(
        local, mesh=mesh, in_specs=(fine, fine, coarse, coarse), out_specs=fine, check_vma=False
    )
```

time: 47.1 us -> 36.3 us (0.77)
  Pallas kernels: 41 us -> 35.1 us
  local copies, waits for them, and re-layouts: 5.9 us -> 1.15 us
    pallas_call x1, Pallas kernels: 41 us -> 35.1 us  [local(): pl.pallas_call(functools.partial(kernel, sizes), out_shape=jax.ShapeDtype...]
    unnamed x9 -> x1, local copies, waits for them, and re-layouts: 5.9 us -> 1.15 us
where the time goes in v2:
time: 36.3 us
  Pallas kernels  35.1 us (97%)
  local copies, waits for them, and re-layouts  1.15 us (3%)
    pallas_call x1, Pallas kernels, local(): pl.pallas_call(functools.partial(kernel, sizes), out_shape=jax.ShapeDtype...  35.1 us
    unnamed x1, local copies, waits for them, and re-layouts  1.15 us

profile of v2, /device:TPU:1, one launch (start us, length us, event | category | flops | bytes accessed | tf_op | source)
XLA Modules:
  0.0 36.3 jit_solution(10329149985186764033)
XLA Ops:
  0.0 35.1 %shard_map.46 = f32[3,16,64,128]{3,2,1,0:T(8,128)S(1)} custom-call(f32[3,16,64,128]{3,2,1,0:T(8,128)} %res_h.1, f32[3,16,64,128]{3,2,1,0:T(8,128)} %ed_h.1, f32[16,64,128]{2,1,0:T(8,128)} %ns_h.1, f32[8,32,64]{2,1,0:T(8,128)} %cs_h.1), custom_call_target="tpu_custom_call" | custom-call | tf_op jit(solution)/shard_map/pallas_call | solution.py:513
  35.1 1.1 %copy.6 = f32[3,16,64,128]{3,2,1,0:T(8,128)} copy(f32[3,16,64,128]{3,2,1,0:T(8,128)S(1)} %shard_map.46) | data formatting | bytes 3145728

commit v3 on v2

--- a/solution.py
+++ b/solution.py
@@ -37,7 +37,7 @@
     rt_g, rt_sc, rt_fg, rt_v1, rt_v2, rt_ab,
     xs_sc, xr_sc, xs_fg, xr_fg, xs_v1, xr_v1, xs_v2, xr_v2, xs_ab, xr_ab,
     ys_sc, yr_sc, ys_fg, yr_fg, ys_v1, yr_v1, ys_v2, yr_v2, ys_ab, yr_ab,
-    ar1, ar2, in_sem, send_sem, recv_sem, ar_send, ar_recv,
+    ar1, ar2, present, in_sem, send_sem, recv_sem, ar_send, ar_recv,
 ):
     _, Z, X, _ = res.shape
     ZC, XC = Z // 2, X // 2
@@ -85,11 +85,15 @@
         {"gx": lax.rem(me["gx"] + dx, sizes["gx"]), "gy": lax.rem(me["gy"] + dy, sizes["gy"])}
         for dx in range(sizes["gx"]) for dy in range(sizes["gy"]) if dx or dy
     ]
+    far = [
+        {"gx": lax.rem(me["gx"] + dx, sizes["gx"]), "gy": lax.rem(me["gy"] + dy, sizes["gy"])}
+        for dx in range(sizes["gx"]) for dy in range(sizes["gy"]) if (dx and dy) or dx == 2 or dy == 2
+    ]
     near = [partners[0], partners[-1], *(
         {"gx": lax.rem(me["gx"] + d, sizes["gx"])} for d in (1, sizes["gx"] - 1)
     ), *({"gy": lax.rem(me["gy"] + d, sizes["gy"])} for d in (1, sizes["gy"] - 1))]
     barrier = pltpu.get_barrier_semaphore()
-    for other in partners + plane:
+    for other in far:
         pl.semaphore_signal(barrier, inc=1, device_id=other, device_id_type=MESH)
 
     zero_plane = jnp.zeros((X, L), F32)
@@ -179,7 +183,20 @@
     xs_sc[1, 1] = face_r[:, 7, :] * (1.0 / face_e[:, 7, :])
     arrived(2)
     ys_sc[2 * third :] = scale_all(2, jnp.zeros((L, L), F32), 0).T[:third]
-    pl.semaphore_wait(barrier, len(partners) + len(plane) + len(near))
+    pl.semaphore_wait(barrier, len(far) + len(near))
+
+    def tell(i):
+        for d in (1 << i, sizes["gz"] - (1 << i)):
+            other = {"gz": lax.rem(me["gz"] + d, sizes["gz"])}
+            pl.semaphore_signal(present.at[i], inc=1, device_id=other, device_id_type=MESH)
+
+    def told(i):
+        pl.semaphore_wait(present.at[i], 2)
+
+    steps = [i for i in range(3) if (1 << i) < sizes["gz"] // 2]
+    tell_0, tell_1, tell_2 = (i in steps for i in range(3))
+    if tell_0:
+        tell(0)
     for m in (sc_yu2, sc_xu1, sc_zu0):
         m.start()
     arrived(3)
@@ -214,6 +231,10 @@
 
     for m in (sc_yu2, sc_xu1, sc_zu0):
         m.wait_recv()
+    if tell_0:
+        told(0)
+    if tell_1:
+        tell(1)
     sc[1, 1 : Z + 1, 7, :] = xr_sc[0, 1]
     low = yr_sc[0, 2 * third :]
     unpack(rt_g, low, jnp.zeros_like(low))
@@ -248,6 +269,10 @@
 
     for m in fg_m:
         m.wait_recv()
+    if tell_1:
+        told(1)
+    if tell_2:
+        tell(2)
     fg[1 : Z + 1, 7, :] = xr_fg[0]
     fg[1 : Z + 1, 8 + X, :] = xr_fg[1]
     unpack(rt_fg, yr_fg[0], yr_fg[1])
@@ -360,7 +385,7 @@
             copy.start()
         return copies
 
-    round1 = spread_round(ar1, partners, 0)
+    round1 = spread_round(ar1, plane, 0)
 
     def prolong(v, wy, j):
         def body(b, _):
@@ -431,7 +456,9 @@
     for copy in round1:
         copy.wait_recv()
     ar2[0] = jnp.sum(ar1[...], axis=0)
-    round2 = spread_round(ar2, plane, len(partners))
+    if tell_2:
+        told(2)
+    round2 = spread_round(ar2, partners, len(plane))
 
     smooth(1)
     smooth(2)
@@ -505,7 +532,7 @@
             v(2, ZC, L), v(2, ZC, L), v(2, ZC, L), v(2, ZC, L), v(3, Z, L), v(3, Z, L),
             v(6 * NB, L), v(2, 6 * NB, L), v(2 * NB, L), v(2, 2 * NB, L),
             v(8, L), v(2, 8, L), v(8, L), v(2, 8, L), v(6 * NB, L), v(6 * NB, L),
-            v(sizes["gz"], 1, L), v(sizes["gx"] * sizes["gy"], 1, L),
+            v(sizes["gx"] * sizes["gy"], 1, L), v(sizes["gz"], 1, L), pltpu.SemaphoreType.REGULAR((3,)),
             pltpu.SemaphoreType.DMA((12,)),
             pltpu.SemaphoreType.DMA((32,)), pltpu.SemaphoreType.DMA((32,)),
             pltpu.SemaphoreType.DMA((n_ar,)), pltpu.SemaphoreType.DMA((n_ar,)),

time: 36.3 us -> 36.5 us (level)
  no operation moved by 1% of the time
where the time goes in v3:
time: 36.5 us; the launch traced here: 36.4 us
  Pallas kernels  35.3 us (97%)
  local copies, waits for them, and re-layouts  1.15 us (3%)
    pallas_call x1, Pallas kernels, local(): pl.pallas_call(functools.partial(kernel, sizes), out_shape=jax.ShapeDtype...  35.3 us
    unnamed x1, local copies, waits for them, and re-layouts  1.15 us

profile of v3, /device:TPU:1, one launch (start us, length us, event | category | flops | bytes accessed | tf_op | source)
XLA Modules:
  0.0 36.4 jit_solution(1827614168483332060)
XLA Ops:
  0.0 35.3 %shard_map.46 = f32[3,16,64,128]{3,2,1,0:T(8,128)S(1)} custom-call(f32[3,16,64,128]{3,2,1,0:T(8,128)} %res_h.1, f32[3,16,64,128]{3,2,1,0:T(8,128)} %ed_h.1, f32[16,64,128]{2,1,0:T(8,128)} %ns_h.1, f32[8,32,64]{2,1,0:T(8,128)} %cs_h.1), custom_call_target="tpu_custom_call" | custom-call | tf_op jit(solution)/shard_map/pallas_call | solution.py:540
  35.3 1.1 %copy.6 = f32[3,16,64,128]{3,2,1,0:T(8,128)} copy(f32[3,16,64,128]{3,2,1,0:T(8,128)S(1)} %shard_map.46) | data formatting | bytes 3145728

commit v4 on v3

--- a/solution.py
+++ b/solution.py
@@ -33,8 +33,9 @@
 
 def kernel(
     sizes, res_h, ed_h, ns_h, cs_h, out,
-    res, ed, ns, cs, sc, fg, tmp, cr, cd, v1, v2, wy1, wy2, a1s, ab, face_e, face_r,
-    rt_g, rt_sc, rt_fg, rt_v1, rt_v2, rt_ab,
+    res, ed, ns, cs, sc, fg, tmp, cr, cd, v1, v2, wy1, wy2, ab, face_e, face_r,
+    rt_g, rt_sc, rt_fg, rt_v1, rt_v2, rt_ab, rt_d,
+    dv, v1b, x2s, x2r, y2s, y2r, cdz, cdxs, cdx, cdys, cdy,
     xs_sc, xr_sc, xs_fg, xr_fg, xs_v1, xr_v1, xs_v2, xr_v2, xs_ab, xr_ab,
     ys_sc, yr_sc, ys_fg, yr_fg, ys_v1, yr_v1, ys_v2, yr_v2, ys_ab, yr_ab,
     ar1, ar2, present, in_sem, send_sem, recv_sem, ar_send, ar_recv,
@@ -47,15 +48,23 @@
     me = {a: lax.axis_index(a) for a in AXES}
     used = []
 
-    def message(src, dst, axis, step):
+    def both(flags):
+        return functools.reduce(jnp.logical_and, flags)
+
+    def message(src, dst, *steps):
         i = len(used)
-        last = sizes[axis] - 1
+        steps = dict(zip(steps[::2], steps[1::2]))
         copy = pltpu.make_async_remote_copy(
             src_ref=src, dst_ref=dst, send_sem=send_sem.at[i], recv_sem=recv_sem.at[i],
-            device_id={axis: me[axis] + step}, device_id_type=MESH,
+            device_id={a: me[a] + d for a, d in steps.items()}, device_id_type=MESH,
         )
-        low, high = me[axis] > 0, me[axis] < last
-        made = Message(copy, *((high, low) if step > 0 else (low, high)))
+        low = {a: me[a] > 0 for a in steps}
+        high = {a: me[a] < sizes[a] - 1 for a in steps}
+        made = Message(
+            copy,
+            both([high[a] if d > 0 else low[a] for a, d in steps.items()]),
+            both([low[a] if d > 0 else high[a] for a, d in steps.items()]),
+        )
         used.append(made)
         return made
 
@@ -87,11 +96,15 @@
     ]
     far = [
         {"gx": lax.rem(me["gx"] + dx, sizes["gx"]), "gy": lax.rem(me["gy"] + dy, sizes["gy"])}
-        for dx in range(sizes["gx"]) for dy in range(sizes["gy"]) if (dx and dy) or dx == 2 or dy == 2
-    ]
-    near = [partners[0], partners[-1], *(
-        {"gx": lax.rem(me["gx"] + d, sizes["gx"])} for d in (1, sizes["gx"] - 1)
-    ), *({"gy": lax.rem(me["gy"] + d, sizes["gy"])} for d in (1, sizes["gy"] - 1))]
+        for dx in range(sizes["gx"]) for dy in range(sizes["gy"]) if dx == 2 or dy == 2
+    ]
+    def at(**steps):
+        return {a: lax.rem(me[a] + d + sizes[a], sizes[a]) for a, d in steps.items()}
+
+    near = [at(**{a: d}) for a in AXES for d in (1, -1)] + [
+        at(**{a: d, b: e})
+        for a, b in (("gx", "gy"), ("gx", "gz"), ("gy", "gz")) for d in (1, -1) for e in (1, -1)
+    ]
     barrier = pltpu.get_barrier_semaphore()
     for other in far:
         pl.semaphore_signal(barrier, inc=1, device_id=other, device_id_type=MESH)
@@ -106,8 +119,11 @@
         fg[z, 8 : 8 + X, :] = zero_plane
     for z in (0, ZC + 1):
         v1[z, 8 : 8 + XC, :] = zero_coarse
-        v2[z, 8 : 8 + XC, :] = zero_coarse
-    for ref in (xr_sc, xr_fg, xr_v1, xr_v2, xr_ab, yr_sc, yr_fg, yr_v1, yr_v2, yr_ab):
+    v2[ZC + 1, 8 : 8 + XC, :] = zero_coarse
+    for ref in (
+        xr_sc, xr_fg, xr_v1, xr_v2, xr_ab, yr_sc, yr_fg, yr_v1, yr_v2, yr_ab,
+        dv, v1b, x2r, y2r, cdz, cdx, cdy,
+    ):
         ref[...] = jnp.zeros(ref.shape, F32)
 
     for other in near:
@@ -228,6 +244,22 @@
         precision=lax.Precision.HIGHEST, preferred_element_type=F32,
     )
     cd[...] = (1.0 / (6.0 + wide)).reshape(ZC, XC, L)
+
+    def pack_coarse(planes):
+        packed = jnp.zeros((L, L), F32)
+        for q in range(NBC):
+            packed = put(packed, planes(PC * q, PC * (q + 1)).reshape(L, L), q)
+        return packed
+
+    cdxs[...] = cd[:, XC - 1, :]
+    cdys[...] = pack_coarse(lambda a, b: cd[a:b]).T[:8]
+    fixed = [
+        message(cd.at[ZC - 1], cdz, "gz", 1),
+        message(cdxs, cdx, "gx", 1),
+        message(cdys, cdy, "gy", 1),
+    ]
+    for m in fixed:
+        m.start()
 
     for m in (sc_yu2, sc_xu1, sc_zu0):
         m.wait_recv()
@@ -304,17 +336,14 @@
         v1[b + 1, 8 : 8 + XC, :] = v
         xs_v1[0, pl.ds(b, 1), :] = v[0:1]
         xs_v1[1, pl.ds(b, 1), :] = v[XC - 1 : XC]
+        x2s[pl.ds(b, 1), :] = v[XC - 2 : XC - 1]
         return 0
 
     each(ZC, direction, 0)
 
-    def coarse_exchange(v, xs, xr, ys, yr):
-        packed = jnp.zeros((L, L), F32)
-        for q in range(NBC):
-            packed = put(packed, v[1 + PC * q : 1 + PC * (q + 1), 8 : 8 + XC, :].reshape(L, L), q)
-        ys[...] = packed.T[:8]
+    def coarse_faces(v, xs, xr, ys, yr):
         mid = pl.ds(8, XC)
-        sent = [
+        return [
             message(ys, yr.at[0], "gy", 1),
             message(ys, yr.at[1], "gy", -1),
             message(xs.at[1], xr.at[0], "gx", 1),
@@ -322,9 +351,6 @@
             message(v.at[ZC, mid, :], v.at[0, mid, :], "gz", 1),
             message(v.at[1, mid, :], v.at[ZC + 1, mid, :], "gz", -1),
         ]
-        for m in sent:
-            m.start()
-        return sent
 
     def coarse_arrive(sent, v, xr, yr, rt):
         for m in sent:
@@ -342,30 +368,108 @@
         n += v[b + 1, 7 : 7 + XC, :] + v[b + 1, 9 : 9 + XC, :]
         return c, n + (w + swap(w))
 
-    v1_m = coarse_exchange(v1, xs_v1, xr_v1, ys_v1, yr_v1)
-    coarse_arrive(v1_m, v1, xr_v1, yr_v1, rt_v1)
+    v1_x = [
+        message(xs_v1.at[1], dv.at[0], "gz", 1, "gx", 1),
+        message(xs_v1.at[0], dv.at[1], "gz", 1, "gx", -1),
+        message(xs_v1.at[1], dv.at[2], "gz", -1, "gx", 1),
+        message(xs_v1.at[1], dv.at[3], "gx", 1, "gy", 1),
+        message(xs_v1.at[1], dv.at[4], "gx", 1, "gy", -1),
+        message(x2s, x2r, "gx", 1),
+        message(v1.at[ZC - 1, pl.ds(8, XC), :], v1b, "gz", 1),
+    ]
+    v1_y = [
+        message(ys_v1, dv.at[5], "gz", 1, "gy", 1),
+        message(ys_v1, dv.at[6], "gz", 1, "gy", -1),
+        message(ys_v1, dv.at[7], "gz", -1, "gy", 1),
+        message(ys_v1, dv.at[8], "gx", 1, "gy", 1),
+        message(ys_v1, dv.at[9], "gx", -1, "gy", 1),
+        message(y2s, y2r, "gy", 1),
+    ]
+    v1_f = coarse_faces(v1, xs_v1, xr_v1, ys_v1, yr_v1)
+    for m in v1_x + v1_f[2:]:
+        m.start()
+    packed = pack_coarse(lambda a, b: v1[1 + a : 1 + b, 8 : 8 + XC, :])
+    for q in range(NBC):
+        block = v1[1 + PC * q : 1 + PC * (q + 1), 8 : 8 + XC, :].reshape(L, L)
+        to = L // 4 + q
+        packed = jnp.where(
+            lax.shift_right_logical(lane2, 1) == to, pltpu.roll(block, 2 * to + 3, 1), packed
+        )
+    turned = packed.T
+    ys_v1[...] = turned[:8]
+    y2s[...] = turned[L // 2 : L // 2 + 8]
+    for m in v1_y + v1_f[:2]:
+        m.start()
+    coarse_arrive(v1_f, v1, xr_v1, yr_v1, rt_v1)
 
     def first(b, sums):
         g1, g2, h11, h12 = sums
         c, n = around(v1, wy1, rt_v1, b)
         r = cr[b]
         a = r - n
-        a1s[b] = a
         w = a * cd[b]
         v2[b + 1, 8 : 8 + XC, :] = w
-        xs_v2[0, pl.ds(b, 1), :] = w[0:1]
-        xs_v2[1, pl.ds(b, 1), :] = w[XC - 1 : XC]
+        xs_v2[pl.ds(b, 1), :] = w[0:1]
         return g1 + c * r, g2 + w * r, h11 + c * a, h12 + w * a
 
     sums = each(ZC, first, (zero_coarse,) * 4)
-    v2_m = coarse_exchange(v2, xs_v2, xr_v2, ys_v2, yr_v2)
-    coarse_arrive(v2_m, v2, xr_v2, yr_v2, rt_v2)
-
-    def second(b, h22):
-        c, n = around(v2, wy2, rt_v2, b)
-        return h22 + c * (a1s[b] - n)
-
-    sums += (each(ZC, second, zero_coarse),)
+    for m in v1_x + v1_y + fixed:
+        m.wait_recv()
+    v1[0, 7:8, :] = dv[0, 7:8, :]
+    v1[0, 8 + XC : 9 + XC, :] = dv[1, 7:8, :]
+    unpack(rt_d, dv[5], dv[6])
+    c = v1[0, 8 : 8 + XC, :]
+    h = halo(rt_d, ((ZC - 1) % PC) * XC, XC, (ZC - 1) // PC)
+    w = jnp.where(evenc, before(c, h, lanec), after(c, h, lanec))
+    n = v1b[...] + v1[1, 8 : 8 + XC, :] + v1[0, 7 : 7 + XC, :] + v1[0, 9 : 9 + XC, :]
+    below_z = c - cdz[...] * (n + (w + swap(w)))
+
+    row, line = iota((8, L), 0), iota((8, L), 1)
+    even = line % 2 == 0
+    c = xr_v1[0]
+    n = x2r[...] + xs_v1[0]
+    n += jnp.where(row == 0, pltpu.roll(dv[0], 1, 0), pltpu.roll(c, 1, 0))
+    n += jnp.where(row == 7, pltpu.roll(dv[2], 7, 0), pltpu.roll(c, 7, 0))
+    low = jnp.where(line == 0, pltpu.roll(dv[3], 1, 1), pltpu.roll(c, 1, 1))
+    high = jnp.where(line == L - 1, pltpu.roll(dv[4], L - 1, 1), pltpu.roll(c, L - 1, 1))
+    w = jnp.where(even, low, high)
+    n += w + jnp.where(even, pltpu.roll(w, L - 1, 1), pltpu.roll(w, 1, 1))
+    below_x = c - cdx[...] * n
+
+    c = yr_v1[0]
+    n = y2r[...] + pltpu.roll(ys_v1[...], 7, 0)
+    down = jnp.where(row >= 2, pltpu.roll(c, 2, 0), pltpu.roll(dv[5], 6, 0))
+    up = jnp.where(row < 2, pltpu.roll(c, 6, 0), pltpu.roll(dv[7], 2, 0))
+    n += pltpu.roll(jnp.where(line < L - XC, c, down), XC, 1)
+    n += pltpu.roll(jnp.where(line >= XC, c, up), L - XC, 1)
+    n += jnp.where(line % XC == 0, pltpu.roll(dv[8], L - XC + 1, 1), pltpu.roll(c, 1, 1))
+    n += jnp.where(line % XC == XC - 1, pltpu.roll(dv[9], XC - 1, 1), pltpu.roll(c, L - 1, 1))
+    below_y = c - cdy[...] * n
+
+    packed = pack_coarse(lambda a, b: v2[1 + a : 1 + b, 8 : 8 + XC, :])
+    ys_v2[...] = packed.T[:8]
+    v2_m = [
+        message(ys_v2, yr_v2, "gy", -1),
+        message(xs_v2, xr_v2, "gx", -1),
+        message(v2.at[1, pl.ds(8, XC), :], v2.at[ZC + 1, pl.ds(8, XC), :], "gz", -1),
+    ]
+    for m in v2_m:
+        m.start()
+    nothing = jnp.zeros((XC, L), F32)
+    v2[0, 8 : 8 + XC, :] = below_z
+    v2[1 : ZC + 1, 7, :] = below_x
+
+    def pairs(b, sums):
+        c = v2[b + 1, 8 : 8 + XC, :]
+        w = jnp.where(evenc, before(c, nothing, lanec), after(c, nothing, lanec))
+        n = v2[b, 8 : 8 + XC, :] + v2[b + 1, 7 : 7 + XC, :]
+        return sums + c * (2.0 * n + 2.0 * w)
+
+    inside = each(ZC, pairs, zero_coarse)
+    side = jnp.where((row == 0) | (row == 2), pltpu.roll(ys_v2[...], 7, 0) * below_y, 0.0)
+    total = sums[3] - inside
+    total = total - jnp.concatenate([4.0 * side, jnp.zeros((XC - 8, L), F32)], axis=0)
+    sums += (total,)
 
     row = jnp.zeros((1, L), F32)
     for i, s in enumerate(sums):
@@ -401,6 +505,18 @@
         each(ZC, body, 0)
 
     prolong(v1, wy1, 1)
+    for m in v2_m:
+        m.wait_recv()
+    v2[1 : ZC + 1, 8 + XC, :] = xr_v2[...]
+    unpack(rt_v2, below_y, yr_v2[...])
+
+    def sides(b, _):
+        c = v2[b + 1, 8 : 8 + XC, :]
+        h = halo(rt_v2, (b % PC) * XC, XC, b // PC)
+        wy2[b] = jnp.where(evenc, before(c, h, lanec), after(c, h, lanec))
+        return 0
+
+    each(ZC, sides, 0)
     prolong(v2, wy2, 2)
 
     def fill(j):
@@ -525,16 +641,18 @@
             v(3, Z + 2, X + 16, L), v(Z + 2, X + 16, L), v(ZC, X, L),
             v(ZC, XC, L), v(ZC, XC, L),
             v(ZC + 2, XC + 16, L), v(ZC + 2, XC + 16, L),
-            v(ZC, XC, L), v(ZC, XC, L), v(ZC, XC, L),
+            v(ZC, XC, L), v(ZC, XC, L),
             v(3, Z + 1, X + 8, L), v(Z, 8, L), v(Z, 8, L),
-            v(L, L), v(L, L), v(L, L), v(L, L), v(L, L), v(L, L),
+            v(L, L), v(L, L), v(L, L), v(L, L), v(L, L), v(L, L), v(L, L),
+            v(10, 8, L), v(XC, L), v(ZC, L), v(ZC, L), v(8, L), v(8, L),
+            v(XC, L), v(ZC, L), v(ZC, L), v(8, L), v(8, L),
             v(2, 3, Z, L), v(2, 3, Z, L), v(2, Z, L), v(2, Z, L),
-            v(2, ZC, L), v(2, ZC, L), v(2, ZC, L), v(2, ZC, L), v(3, Z, L), v(3, Z, L),
+            v(2, ZC, L), v(2, ZC, L), v(ZC, L), v(ZC, L), v(3, Z, L), v(3, Z, L),
             v(6 * NB, L), v(2, 6 * NB, L), v(2 * NB, L), v(2, 2 * NB, L),
-            v(8, L), v(2, 8, L), v(8, L), v(2, 8, L), v(6 * NB, L), v(6 * NB, L),
+            v(8, L), v(2, 8, L), v(8, L), v(8, L), v(6 * NB, L), v(6 * NB, L),
             v(sizes["gx"] * sizes["gy"], 1, L), v(sizes["gz"], 1, L), pltpu.SemaphoreType.REGULAR((3,)),
             pltpu.SemaphoreType.DMA((12,)),
-            pltpu.SemaphoreType.DMA((32,)), pltpu.SemaphoreType.DMA((32,)),
+            pltpu.SemaphoreType.DMA((56,)), pltpu.SemaphoreType.DMA((56,)),
             pltpu.SemaphoreType.DMA((n_ar,)), pltpu.SemaphoreType.DMA((n_ar,)),
         ]
         return pl.pallas_call(

time: 36.5 us -> 34.6 us (0.948)
  Pallas kernels: 35.3 us -> 33.4 us
    pallas_call x1, Pallas kernels: 35.3 us -> 33.4 us  [local(): pl.pallas_call(functools.partial(kernel, sizes), out_shape=jax.ShapeDtype...]
where the time goes in v4:
time: 34.6 us
  Pallas kernels  33.4 us (97%)
  local copies, waits for them, and re-layouts  1.15 us (3%)
    pallas_call x1, Pallas kernels, local(): pl.pallas_call(functools.partial(kernel, sizes), out_shape=jax.ShapeDtype...  33.4 us
    unnamed x1, local copies, waits for them, and re-layouts  1.15 us

profile of v4, /device:TPU:1, one launch (start us, length us, event | category | flops | bytes accessed | tf_op | source)
XLA Modules:
  0.0 34.6 jit_solution(203564660567670701)
XLA Ops:
  0.0 33.4 %shard_map.46 = f32[3,16,64,128]{3,2,1,0:T(8,128)S(1)} custom-call(f32[3,16,64,128]{3,2,1,0:T(8,128)} %res_h.1, f32[3,16,64,128]{3,2,1,0:T(8,128)} %ed_h.1, f32[16,64,128]{2,1,0:T(8,128)} %ns_h.1, f32[8,32,64]{2,1,0:T(8,128)} %cs_h.1), custom_call_target="tpu_custom_call" | custom-call | tf_op jit(solution)/shard_map/pallas_call | solution.py:658
  33.4 1.1 %copy.6 = f32[3,16,64,128]{3,2,1,0:T(8,128)} copy(f32[3,16,64,128]{3,2,1,0:T(8,128)S(1)} %shard_map.46) | data formatting | bytes 3145728

commit v5 on v4

--- a/solution.py
+++ b/solution.py
@@ -94,20 +94,11 @@
         {"gx": lax.rem(me["gx"] + dx, sizes["gx"]), "gy": lax.rem(me["gy"] + dy, sizes["gy"])}
         for dx in range(sizes["gx"]) for dy in range(sizes["gy"]) if dx or dy
     ]
-    far = [
-        {"gx": lax.rem(me["gx"] + dx, sizes["gx"]), "gy": lax.rem(me["gy"] + dy, sizes["gy"])}
-        for dx in range(sizes["gx"]) for dy in range(sizes["gy"]) if dx == 2 or dy == 2
-    ]
     def at(**steps):
         return {a: lax.rem(me[a] + d + sizes[a], sizes[a]) for a, d in steps.items()}
 
-    near = [at(**{a: d}) for a in AXES for d in (1, -1)] + [
-        at(**{a: d, b: e})
-        for a, b in (("gx", "gy"), ("gx", "gz"), ("gy", "gz")) for d in (1, -1) for e in (1, -1)
-    ]
+    near = [at(**{a: d}) for a in AXES for d in (1, -1)]
     barrier = pltpu.get_barrier_semaphore()
-    for other in far:
-        pl.semaphore_signal(barrier, inc=1, device_id=other, device_id_type=MESH)
 
     zero_plane = jnp.zeros((X, L), F32)
     zero_coarse = jnp.zeros((XC, L), F32)
@@ -199,22 +190,25 @@
     xs_sc[1, 1] = face_r[:, 7, :] * (1.0 / face_e[:, 7, :])
     arrived(2)
     ys_sc[2 * third :] = scale_all(2, jnp.zeros((L, L), F32), 0).T[:third]
-    pl.semaphore_wait(barrier, len(far) + len(near))
+    pl.semaphore_wait(barrier, len(near))
+
+    known = [
+        near,
+        [at(**{a: d}) for a in AXES for d in (2, -2) if sizes[a] > 4 or (sizes[a] == 4 and d > 0)],
+        [at(gz=d) for d in (4, -4) if sizes["gz"] > 8],
+    ]
 
     def tell(i):
-        for d in (1 << i, sizes["gz"] - (1 << i)):
-            other = {"gz": lax.rem(me["gz"] + d, sizes["gz"])}
+        for other in known[i]:
             pl.semaphore_signal(present.at[i], inc=1, device_id=other, device_id_type=MESH)
 
     def told(i):
-        pl.semaphore_wait(present.at[i], 2)
-
-    steps = [i for i in range(3) if (1 << i) < sizes["gz"] // 2]
-    tell_0, tell_1, tell_2 = (i in steps for i in range(3))
-    if tell_0:
-        tell(0)
+        if known[i]:
+            pl.semaphore_wait(present.at[i], len(known[i]))
+
     for m in (sc_yu2, sc_xu1, sc_zu0):
         m.start()
+    tell(0)
     arrived(3)
     packed = scale_all(1, jnp.zeros((L, L), F32), NB)
     arrived(4)
@@ -263,10 +257,8 @@
 
     for m in (sc_yu2, sc_xu1, sc_zu0):
         m.wait_recv()
-    if tell_0:
-        told(0)
-    if tell_1:
-        tell(1)
+    told(0)
+    tell(1)
     sc[1, 1 : Z + 1, 7, :] = xr_sc[0, 1]
     low = yr_sc[0, 2 * third :]
     unpack(rt_g, low, jnp.zeros_like(low))
@@ -301,10 +293,8 @@
 
     for m in fg_m:
         m.wait_recv()
-    if tell_1:
-        told(1)
-    if tell_2:
-        tell(2)
+    told(1)
+    tell(2)
     fg[1 : Z + 1, 7, :] = xr_fg[0]
     fg[1 : Z + 1, 8 + X, :] = xr_fg[1]
     unpack(rt_fg, yr_fg[0], yr_fg[1])
@@ -505,44 +495,6 @@
         each(ZC, body, 0)
 
     prolong(v1, wy1, 1)
-    for m in v2_m:
-        m.wait_recv()
-    v2[1 : ZC + 1, 8 + XC, :] = xr_v2[...]
-    unpack(rt_v2, below_y, yr_v2[...])
-
-    def sides(b, _):
-        c = v2[b + 1, 8 : 8 + XC, :]
-        h = halo(rt_v2, (b % PC) * XC, XC, b // PC)
-        wy2[b] = jnp.where(evenc, before(c, h, lanec), after(c, h, lanec))
-        return 0
-
-    each(ZC, sides, 0)
-    prolong(v2, wy2, 2)
-
-    def fill(j):
-        def body(b, packed):
-            block = []
-            for p in range(2):
-                z = 2 * b + p
-                x = ab[j, z, 0:X, :]
-                xs_ab[j, pl.ds(z, 1), :] = x[0:1]
-                block.append(x)
-            return put(packed, jnp.concatenate(block, axis=0), j * NB + b)
-
-        return body
-
-    packed = jnp.zeros((L, L), F32)
-    for j in range(3):
-        packed = each(NB, fill(j), packed)
-    ys_ab[...] = packed.T[: 6 * NB]
-    ab_m = [
-        message(ab.at[:, 0, pl.ds(0, X), :], ab.at[:, Z, pl.ds(0, X), :], "gz", -1),
-        message(xs_ab, xr_ab, "gx", -1),
-        message(ys_ab, yr_ab, "gy", -1),
-    ]
-    for m in ab_m:
-        m.start()
-
     def smooth(k):
         def body(b, _):
             for p in range(2):
@@ -572,9 +524,46 @@
     for copy in round1:
         copy.wait_recv()
     ar2[0] = jnp.sum(ar1[...], axis=0)
-    if tell_2:
-        told(2)
+    told(2)
     round2 = spread_round(ar2, partners, len(plane))
+
+    for m in v2_m:
+        m.wait_recv()
+    v2[1 : ZC + 1, 8 + XC, :] = xr_v2[...]
+    unpack(rt_v2, below_y, yr_v2[...])
+
+    def sides(b, _):
+        c = v2[b + 1, 8 : 8 + XC, :]
+        h = halo(rt_v2, (b % PC) * XC, XC, b // PC)
+        wy2[b] = jnp.where(evenc, before(c, h, lanec), after(c, h, lanec))
+        return 0
+
+    each(ZC, sides, 0)
+    prolong(v2, wy2, 2)
+
+    def fill(j):
+        def body(b, packed):
+            block = []
+            for p in range(2):
+                z = 2 * b + p
+                x = ab[j, z, 0:X, :]
+                xs_ab[j, pl.ds(z, 1), :] = x[0:1]
+                block.append(x)
+            return put(packed, jnp.concatenate(block, axis=0), j * NB + b)
+
+        return body
+
+    packed = jnp.zeros((L, L), F32)
+    for j in range(3):
+        packed = each(NB, fill(j), packed)
+    ys_ab[...] = packed.T[: 6 * NB]
+    ab_m = [
+        message(ab.at[:, 0, pl.ds(0, X), :], ab.at[:, Z, pl.ds(0, X), :], "gz", -1),
+        message(xs_ab, xr_ab, "gx", -1),
+        message(ys_ab, yr_ab, "gy", -1),
+    ]
+    for m in ab_m:
+        m.start()
 
     smooth(1)
     smooth(2)

time: 34.6 us -> 34.1 us (0.986)
  Pallas kernels: 33.4 us -> 32.8 us
    pallas_call x1, Pallas kernels: 33.4 us -> 32.8 us  [local(): pl.pallas_call(functools.partial(kernel, sizes), out_shape=jax.ShapeDtype...]
where the time goes in v5:
time: 34.1 us; the launch traced here: 34 us
  Pallas kernels  32.8 us (96%)
  local copies, waits for them, and re-layouts  1.15 us (3%)
    pallas_call x1, Pallas kernels, local(): pl.pallas_call(functools.partial(kernel, sizes), out_shape=jax.ShapeDtype...  32.8 us
    unnamed x1, local copies, waits for them, and re-layouts  1.15 us

profile of v5, /device:TPU:1, one launch (start us, length us, event | category | flops | bytes accessed | tf_op | source)
XLA Modules:
  0.0 34.0 jit_solution(18071468453655719104)
XLA Ops:
  0.0 32.8 %shard_map.46 = f32[3,16,64,128]{3,2,1,0:T(8,128)S(1)} custom-call(f32[3,16,64,128]{3,2,1,0:T(8,128)} %res_h.1, f32[3,16,64,128]{3,2,1,0:T(8,128)} %ed_h.1, f32[16,64,128]{2,1,0:T(8,128)} %ns_h.1, f32[8,32,64]{2,1,0:T(8,128)} %cs_h.1), custom_call_target="tpu_custom_call" | custom-call | tf_op jit(solution)/shard_map/pallas_call | solution.py:647
  32.8 1.1 %copy.6 = f32[3,16,64,128]{3,2,1,0:T(8,128)} copy(f32[3,16,64,128]{3,2,1,0:T(8,128)S(1)} %shard_map.46) | data formatting | bytes 3145728

commit v6 on v5

--- a/solution.py
+++ b/solution.py
@@ -38,7 +38,7 @@
     dv, v1b, x2s, x2r, y2s, y2r, cdz, cdxs, cdx, cdys, cdy,
     xs_sc, xr_sc, xs_fg, xr_fg, xs_v1, xr_v1, xs_v2, xr_v2, xs_ab, xr_ab,
     ys_sc, yr_sc, ys_fg, yr_fg, ys_v1, yr_v1, ys_v2, yr_v2, ys_ab, yr_ab,
-    ar1, ar2, present, in_sem, send_sem, recv_sem, ar_send, ar_recv,
+    arow, ar1, ar2, present, in_sem, send_sem, recv_sem, ar_send, ar_recv, out_send, out_recv,
 ):
     _, Z, X, _ = res.shape
     ZC, XC = Z // 2, X // 2
@@ -46,6 +46,7 @@
     PC = L // XC
     NBC = ZC // PC
     me = {a: lax.axis_index(a) for a in AXES}
+    core = lax.rem(me["gz"], 2)
     used = []
 
     def both(flags):
@@ -83,39 +84,35 @@
     ]
     load_ns = pltpu.make_async_copy(ns_h, ns, in_sem.at[10])
     load_cs = pltpu.make_async_copy(cs_h, cs, in_sem.at[11])
-    for pair in loads:
+    for pair in loads[:3]:
         for copy in pair:
             copy.start()
-    load_ns.start()
-    load_cs.start()
-
-    partners = [{"gz": lax.rem(me["gz"] + d, sizes["gz"])} for d in range(1, sizes["gz"])]
-    plane = [
-        {"gx": lax.rem(me["gx"] + dx, sizes["gx"]), "gy": lax.rem(me["gy"] + dy, sizes["gy"])}
-        for dx in range(sizes["gx"]) for dy in range(sizes["gy"]) if dx or dy
-    ]
+
     def at(**steps):
         return {a: lax.rem(me[a] + d + sizes[a], sizes[a]) for a, d in steps.items()}
 
     near = [at(**{a: d}) for a in AXES for d in (1, -1)]
     barrier = pltpu.get_barrier_semaphore()
 
-    zero_plane = jnp.zeros((X, L), F32)
     zero_coarse = jnp.zeros((XC, L), F32)
-    for k in range(3):
+
+    @pl.when(me["gz"] >= 0)
+    def _():
+        zero_plane = jnp.zeros((X, L), F32)
+        for k in range(3):
+            for z in (0, Z + 1):
+                sc[k, z, 8 : 8 + X, :] = zero_plane
+            ab[k, Z, 0:X, :] = zero_plane
         for z in (0, Z + 1):
-            sc[k, z, 8 : 8 + X, :] = zero_plane
-        ab[k, Z, 0:X, :] = zero_plane
-    for z in (0, Z + 1):
-        fg[z, 8 : 8 + X, :] = zero_plane
-    for z in (0, ZC + 1):
-        v1[z, 8 : 8 + XC, :] = zero_coarse
-    v2[ZC + 1, 8 : 8 + XC, :] = zero_coarse
-    for ref in (
-        xr_sc, xr_fg, xr_v1, xr_v2, xr_ab, yr_sc, yr_fg, yr_v1, yr_v2, yr_ab,
-        dv, v1b, x2r, y2r, cdz, cdx, cdy,
-    ):
-        ref[...] = jnp.zeros(ref.shape, F32)
+            fg[z, 8 : 8 + X, :] = zero_plane
+        for z in (0, ZC + 1):
+            v1[z, 8 : 8 + XC, :] = zero_coarse
+        v2[ZC + 1, 8 : 8 + XC, :] = zero_coarse
+        for ref in (
+            xr_sc, xr_fg, xr_v1, xr_v2, xr_ab, yr_sc, yr_fg, yr_v1, yr_v2, yr_ab,
+            dv, v1b, x2r, y2r, cdz, cdx, cdy,
+        ):
+            ref[...] = jnp.zeros(ref.shape, F32)
 
     for other in near:
         pl.semaphore_signal(barrier, inc=1, device_id=other, device_id_type=MESH)
@@ -189,13 +186,18 @@
     arrived(1)
     xs_sc[1, 1] = face_r[:, 7, :] * (1.0 / face_e[:, 7, :])
     arrived(2)
+    for pair in loads[3:]:
+        for copy in pair:
+            copy.start()
+    load_ns.start()
+    load_cs.start()
     ys_sc[2 * third :] = scale_all(2, jnp.zeros((L, L), F32), 0).T[:third]
     pl.semaphore_wait(barrier, len(near))
 
     known = [
         near,
         [at(**{a: d}) for a in AXES for d in (2, -2) if sizes[a] > 4 or (sizes[a] == 4 and d > 0)],
-        [at(gz=d) for d in (4, -4) if sizes["gz"] > 8],
+        [at(gz=d) for d in (4, -4) if sizes["gz"] > 8] + [{"gz": me["gz"] + 1 - 2 * core}],
     ]
 
     def tell(i):
@@ -258,7 +260,6 @@
     for m in (sc_yu2, sc_xu1, sc_zu0):
         m.wait_recv()
     told(0)
-    tell(1)
     sc[1, 1 : Z + 1, 7, :] = xr_sc[0, 1]
     low = yr_sc[0, 2 * third :]
     unpack(rt_g, low, jnp.zeros_like(low))
@@ -290,11 +291,11 @@
     ]
     for m in fg_m:
         m.start()
+    tell(1)
 
     for m in fg_m:
         m.wait_recv()
     told(1)
-    tell(2)
     fg[1 : Z + 1, 7, :] = xr_fg[0]
     fg[1 : Z + 1, 8 + X, :] = xr_fg[1]
     unpack(rt_fg, yr_fg[0], yr_fg[1])
@@ -390,6 +391,7 @@
     y2s[...] = turned[L // 2 : L // 2 + 8]
     for m in v1_y + v1_f[:2]:
         m.start()
+    tell(2)
     coarse_arrive(v1_f, v1, xr_v1, yr_v1, rt_v1)
 
     def first(b, sums):
@@ -465,21 +467,40 @@
     for i, s in enumerate(sums):
         one = jnp.sum(jnp.sum(s, axis=0, keepdims=True), axis=1, keepdims=True)
         row = jnp.where(iota((1, L), 1) == i, one, row)
-    ar1[0] = row
-
-    def spread_round(buf, others, base):
-        copies = [
-            pltpu.make_async_remote_copy(
-                src_ref=buf.at[0], dst_ref=buf.at[d + 1], send_sem=ar_send.at[base + d],
-                recv_sem=ar_recv.at[base + d], device_id=other, device_id_type=MESH,
-            )
-            for d, other in enumerate(others)
+    arow[...] = row
+
+    spots = [(dx, dy) for dx in range(sizes["gx"]) for dy in range(sizes["gy"])]
+    n_spots, n_chips = len(spots), sizes["gz"] // 2
+
+    def remote(src, dst, i, j, sends, receives, other):
+        return pltpu.make_async_remote_copy(
+            src_ref=src, dst_ref=dst, send_sem=sends.at[i], recv_sem=receives.at[j],
+            device_id=other, device_id_type=MESH,
+        )
+
+    gather = [
+        [
+            remote(arow, ar1.at[n_spots * c + i], i, n_spots * c + i, ar_send, ar_recv, at(gx=dx, gy=dy, gz=1 - c))
+            for i, (dx, dy) in enumerate(spots) if c == 0 or i > 0
         ]
-        for copy in copies:
+        for c in range(2)
+    ]
+    scatter = [
+        remote(ar2.at[0], ar2.at[d], 2 * d + c, d, out_send, out_recv, at(gz=2 * d - c))
+        for d in range(n_chips) for c in range(2) if d or c
+    ]
+    told(2)
+
+    @pl.when(core == 0)
+    def _():
+        for copy in gather[0]:
             copy.start()
-        return copies
-
-    round1 = spread_round(ar1, plane, 0)
+
+    @pl.when(core == 1)
+    def _():
+        for copy in gather[1]:
+            copy.start()
+        ar1[n_spots] = arow[...]
 
     def prolong(v, wy, j):
         def body(b, _):
@@ -521,11 +542,13 @@
     fill_rows()
     smooth(0)
 
-    for copy in round1:
-        copy.wait_recv()
-    ar2[0] = jnp.sum(ar1[...], axis=0)
-    told(2)
-    round2 = spread_round(ar2, partners, len(plane))
+    @pl.when(core == 1)
+    def _():
+        for copy in gather[0] + gather[1]:
+            copy.wait_recv()
+        ar2[0] = jnp.sum(ar1[...], axis=0)
+        for copy in scatter:
+            copy.start()
 
     for m in v2_m:
         m.wait_recv()
@@ -591,8 +614,13 @@
     gradient(1, res, False)
     gradient(2, ed, False)
 
-    for copy in round2:
-        copy.wait_recv()
+    for d in range(1, n_chips):
+        scatter[2 * d].wait_recv()
+
+    @pl.when(core == 0)
+    def _():
+        scatter[0].wait_recv()
+
     total = jnp.sum(ar2[...], axis=0)
     g1, g2, h11, h12, h22 = (
         jnp.sum(jnp.where(iota((1, L), 1) == i, total, 0.0), axis=1, keepdims=True) for i in range(5)
@@ -609,13 +637,21 @@
 
     for m in used:
         m.wait_send()
-    for copy in round1 + round2:
-        copy.wait_send()
+
+    @pl.when(core == 0)
+    def _():
+        for copy in gather[0]:
+            copy.wait_send()
+
+    @pl.when(core == 1)
+    def _():
+        for copy in gather[1] + scatter:
+            copy.wait_send()
 
 
 def solution(mesh):
     sizes = dict(mesh.shape)
-    n_ar = sizes["gz"] - 1 + sizes["gx"] * sizes["gy"] - 1
+    n_spots, n_chips = sizes["gx"] * sizes["gy"], sizes["gz"] // 2
 
     def local(residual, edge_diag, node_shift, coarse_shift):
         _, Z, X, Y = residual.shape
@@ -639,10 +675,11 @@
             v(2, ZC, L), v(2, ZC, L), v(ZC, L), v(ZC, L), v(3, Z, L), v(3, Z, L),
             v(6 * NB, L), v(2, 6 * NB, L), v(2 * NB, L), v(2, 2 * NB, L),
             v(8, L), v(2, 8, L), v(8, L), v(8, L), v(6 * NB, L), v(6 * NB, L),
-            v(sizes["gx"] * sizes["gy"], 1, L), v(sizes["gz"], 1, L), pltpu.SemaphoreType.REGULAR((3,)),
+            v(1, L), v(2 * n_spots, 1, L), v(n_chips, 1, L), pltpu.SemaphoreType.REGULAR((3,)),
             pltpu.SemaphoreType.DMA((12,)),
             pltpu.SemaphoreType.DMA((56,)), pltpu.SemaphoreType.DMA((56,)),
-            pltpu.SemaphoreType.DMA((n_ar,)), pltpu.SemaphoreType.DMA((n_ar,)),
+            pltpu.SemaphoreType.DMA((n_spots,)), pltpu.SemaphoreType.DMA((2 * n_spots,)),
+            pltpu.SemaphoreType.DMA((2 * n_chips,)), pltpu.SemaphoreType.DMA((n_chips,)),
         ]
         return pl.pallas_call(
             functools.partial(kernel, sizes),

time: 34.1 us -> 33.2 us (0.974)
  Pallas kernels: 32.8 us -> 31.9 us
    pallas_call x1, Pallas kernels: 32.8 us -> 31.9 us  [local(): pl.pallas_call(functools.partial(kernel, sizes), out_shape=jax.ShapeDtype...]
where the time goes in v6:
time: 33.2 us; the launch traced here: 33.1 us
  Pallas kernels  31.9 us (96%)
  local copies, waits for them, and re-layouts  1.15 us (3%)
    pallas_call x1, Pallas kernels, local(): pl.pallas_call(functools.partial(kernel, sizes), out_shape=jax.ShapeDtype...  31.9 us
    unnamed x1, local copies, waits for them, and re-layouts  1.15 us

profile of v6, /device:TPU:1, one launch (start us, length us, event | category | flops | bytes accessed | tf_op | source)
XLA Modules:
  0.0 33.1 jit_solution(17095979391035279558)
XLA Ops:
  0.0 31.9 %shard_map.46 = f32[3,16,64,128]{3,2,1,0:T(8,128)S(1)} custom-call(f32[3,16,64,128]{3,2,1,0:T(8,128)} %res_h.1, f32[3,16,64,128]{3,2,1,0:T(8,128)} %ed_h.1, f32[16,64,128]{2,1,0:T(8,128)} %ns_h.1, f32[8,32,64]{2,1,0:T(8,128)} %cs_h.1), custom_call_target="tpu_custom_call" | custom-call | tf_op jit(solution)/shard_map/pallas_call | solution.py:684
  31.9 1.1 %copy.6 = f32[3,16,64,128]{3,2,1,0:T(8,128)} copy(f32[3,16,64,128]{3,2,1,0:T(8,128)S(1)} %shard_map.46) | data formatting | bytes 3145728

commit v7 on v6

--- a/solution.py
+++ b/solution.py
@@ -139,8 +139,8 @@
         mixed = jnp.where(iota((n, L), 0) % 2 == 1, pltpu.roll(low, 1, 0), pltpu.roll(high, n - 1, 0))
         rt[...] = jnp.concatenate([mixed, jnp.zeros((L - n, L), F32)], axis=0).T
 
-    def each(n, body, init):
-        return lax.fori_loop(0, n, body, init, unroll=True)
+    def each(n, body, init, start=0):
+        return lax.fori_loop(start, n, body, init, unroll=True)
 
     inner = pl.ds(8, X)
     third = 2 * NB
@@ -279,18 +279,24 @@
             block.append(g)
         return put(packed, jnp.concatenate(block, axis=0), b)
 
-    packed = each(NB, guess, jnp.zeros((L, L), F32))
-    ys_fg[...] = packed.T[: 2 * NB]
+    fg_z = [
+        message(fg.at[Z, inner, :], fg.at[0, inner, :], "gz", 1),
+        message(fg.at[1, inner, :], fg.at[Z + 1, inner, :], "gz", -1),
+    ]
     fg_m = [
         message(ys_fg, yr_fg.at[0], "gy", 1),
         message(ys_fg, yr_fg.at[1], "gy", -1),
         message(xs_fg.at[1], xr_fg.at[0], "gx", 1),
         message(xs_fg.at[0], xr_fg.at[1], "gx", -1),
-        message(fg.at[Z, inner, :], fg.at[0, inner, :], "gz", 1),
-        message(fg.at[1, inner, :], fg.at[Z + 1, inner, :], "gz", -1),
-    ]
+    ]
+    packed = guess(NB - 1, guess(0, jnp.zeros((L, L), F32)))
+    for m in fg_z:
+        m.start()
+    packed = each(NB - 1, guess, packed, 1)
+    ys_fg[...] = packed.T[: 2 * NB]
     for m in fg_m:
         m.start()
+    fg_m += fg_z
     tell(1)
 
     for m in fg_m:
@@ -317,8 +323,6 @@
         tmp[b] = total
         return 0
 
-    each(ZC, restrict, 0)
-
     def direction(b, _):
         u = tmp[b, pl.ds(0, XC, 2), :] + tmp[b, pl.ds(1, XC, 2), :]
         u = u + swap(u)
@@ -330,8 +334,6 @@
         x2s[pl.ds(b, 1), :] = v[XC - 2 : XC - 1]
         return 0
 
-    each(ZC, direction, 0)
-
     def coarse_faces(v, xs, xr, ys, yr):
         mid = pl.ds(8, XC)
         return [
@@ -377,7 +379,16 @@
         message(y2s, y2r, "gy", 1),
     ]
     v1_f = coarse_faces(v1, xs_v1, xr_v1, ys_v1, yr_v1)
-    for m in v1_x + v1_f[2:]:
+    early = v1_f[4:] + v1_x[6:]
+    for b in (0, ZC - 1, ZC - 2):
+        restrict(b, 0)
+    for b in (0, ZC - 1, ZC - 2):
+        direction(b, 0)
+    for m in early:
+        m.start()
+    each(ZC - 2, restrict, 0, 1)
+    each(ZC - 2, direction, 0, 1)
+    for m in v1_x[:6] + v1_f[2:4]:
         m.start()
     packed = pack_coarse(lambda a, b: v1[1 + a : 1 + b, 8 : 8 + XC, :])
     for q in range(NBC):
@@ -438,6 +449,60 @@
     n += jnp.where(line % XC == XC - 1, pltpu.roll(dv[9], XC - 1, 1), pltpu.roll(c, L - 1, 1))
     below_y = c - cdy[...] * n
 
+    unpack(rt_d, 2.0 * below_y, jnp.zeros((8, L), F32))
+    nothing = jnp.zeros((XC, L), F32)
+    v2[0, 8 : 8 + XC, :] = below_z
+    v2[1 : ZC + 1, 7, :] = below_x
+
+    def pairs(b, sums):
+        c = v2[b + 1, 8 : 8 + XC, :]
+        h = halo(rt_d, (b % PC) * XC, XC, b // PC)
+        w = jnp.where(evenc, before(c, h, lanec), after(c, nothing, lanec))
+        n = v2[b, 8 : 8 + XC, :] + v2[b + 1, 7 : 7 + XC, :]
+        return sums + c * (2.0 * n + 2.0 * w)
+
+    inside = each(ZC, pairs, zero_coarse)
+    sums += (sums[3] - inside,)
+
+    row = jnp.zeros((1, L), F32)
+    for i, s in enumerate(sums):
+        one = jnp.sum(jnp.sum(s, axis=0, keepdims=True), axis=1, keepdims=True)
+        row = jnp.where(iota((1, L), 1) == i, one, row)
+    arow[...] = row
+
+    spots = [(dx, dy) for dx in range(sizes["gx"]) for dy in range(sizes["gy"])]
+    n_spots, n_chips = len(spots), sizes["gz"] // 2
+
+    def remote(src, dst, i, j, sends, receives, other):
+        return pltpu.make_async_remote_copy(
+            src_ref=src, dst_ref=dst, send_sem=sends.at[i], recv_sem=receives.at[j],
+            device_id=other, device_id_type=MESH,
+        )
+
+    gather = [
+        [
+            remote(arow, ar1.at[n_spots * c + i], i, n_spots * c + i, ar_send, ar_recv, at(gx=dx, gy=dy, gz=1 - c))
+            for i, (dx, dy) in enumerate(spots) if c == 0 or i > 0
+        ]
+        for c in range(2)
+    ]
+    scatter = [
+        remote(ar2.at[0], ar2.at[d], 2 * d + c, d, out_send, out_recv, at(gz=2 * d - c))
+        for d in range(n_chips) for c in range(2) if d or c
+    ]
+    told(2)
+
+    @pl.when(core == 0)
+    def _():
+        for copy in gather[0]:
+            copy.start()
+
+    @pl.when(core == 1)
+    def _():
+        for copy in gather[1]:
+            copy.start()
+        ar1[n_spots] = arow[...]
+
     packed = pack_coarse(lambda a, b: v2[1 + a : 1 + b, 8 : 8 + XC, :])
     ys_v2[...] = packed.T[:8]
     v2_m = [
@@ -447,60 +512,6 @@
     ]
     for m in v2_m:
         m.start()
-    nothing = jnp.zeros((XC, L), F32)
-    v2[0, 8 : 8 + XC, :] = below_z
-    v2[1 : ZC + 1, 7, :] = below_x
-
-    def pairs(b, sums):
-        c = v2[b + 1, 8 : 8 + XC, :]
-        w = jnp.where(evenc, before(c, nothing, lanec), after(c, nothing, lanec))
-        n = v2[b, 8 : 8 + XC, :] + v2[b + 1, 7 : 7 + XC, :]
-        return sums + c * (2.0 * n + 2.0 * w)
-
-    inside = each(ZC, pairs, zero_coarse)
-    side = jnp.where((row == 0) | (row == 2), pltpu.roll(ys_v2[...], 7, 0) * below_y, 0.0)
-    total = sums[3] - inside
-    total = total - jnp.concatenate([4.0 * side, jnp.zeros((XC - 8, L), F32)], axis=0)
-    sums += (total,)
-
-    row = jnp.zeros((1, L), F32)
-    for i, s in enumerate(sums):
-        one = jnp.sum(jnp.sum(s, axis=0, keepdims=True), axis=1, keepdims=True)
-        row = jnp.where(iota((1, L), 1) == i, one, row)
-    arow[...] = row
-
-    spots = [(dx, dy) for dx in range(sizes["gx"]) for dy in range(sizes["gy"])]
-    n_spots, n_chips = len(spots), sizes["gz"] // 2
-
-    def remote(src, dst, i, j, sends, receives, other):
-        return pltpu.make_async_remote_copy(
-            src_ref=src, dst_ref=dst, send_sem=sends.at[i], recv_sem=receives.at[j],
-            device_id=other, device_id_type=MESH,
-        )
-
-    gather = [
-        [
-            remote(arow, ar1.at[n_spots * c + i], i, n_spots * c + i, ar_send, ar_recv, at(gx=dx, gy=dy, gz=1 - c))
-            for i, (dx, dy) in enumerate(spots) if c == 0 or i > 0
-        ]
-        for c in range(2)
-    ]
-    scatter = [
-        remote(ar2.at[0], ar2.at[d], 2 * d + c, d, out_send, out_recv, at(gz=2 * d - c))
-        for d in range(n_chips) for c in range(2) if d or c
-    ]
-    told(2)
-
-    @pl.when(core == 0)
-    def _():
-        for copy in gather[0]:
-            copy.start()
-
-    @pl.when(core == 1)
-    def _():
-        for copy in gather[1]:
-            copy.start()
-        ar1[n_spots] = arow[...]
 
     def prolong(v, wy, j):
         def body(b, _):

time: 33.2 us -> 32.5 us (0.979)
  Pallas kernels: 31.9 us -> 31.3 us
    pallas_call x1, Pallas kernels: 31.9 us -> 31.3 us  [local(): pl.pallas_call(functools.partial(kernel, sizes), out_shape=jax.ShapeDtype...]
where the time goes in v7:
time: 32.5 us; the launch traced here: 32.4 us
  Pallas kernels  31.3 us (96%)
  local copies, waits for them, and re-layouts  1.15 us (4%)
    pallas_call x1, Pallas kernels, local(): pl.pallas_call(functools.partial(kernel, sizes), out_shape=jax.ShapeDtype...  31.3 us
    unnamed x1, local copies, waits for them, and re-layouts  1.15 us

profile of v7, /device:TPU:1, one launch (start us, length us, event | category | flops | bytes accessed | tf_op | source)
XLA Modules:
  0.0 32.4 jit_solution(17872846663338934350)
XLA Ops:
  0.0 31.3 %shard_map.46 = f32[3,16,64,128]{3,2,1,0:T(8,128)S(1)} custom-call(f32[3,16,64,128]{3,2,1,0:T(8,128)} %res_h.1, f32[3,16,64,128]{3,2,1,0:T(8,128)} %ed_h.1, f32[16,64,128]{2,1,0:T(8,128)} %ns_h.1, f32[8,32,64]{2,1,0:T(8,128)} %cs_h.1), custom_call_target="tpu_custom_call" | custom-call | tf_op jit(solution)/shard_map/pallas_call | solution.py:695
  31.3 1.1 %copy.6 = f32[3,16,64,128]{3,2,1,0:T(8,128)} copy(f32[3,16,64,128]{3,2,1,0:T(8,128)S(1)} %shard_map.46) | data formatting | bytes 3145728

commit v8 on v7

--- a/solution.py
+++ b/solution.py
@@ -185,6 +185,24 @@
     scale(0, Z - 1)
     arrived(1)
     xs_sc[1, 1] = face_r[:, 7, :] * (1.0 / face_e[:, 7, :])
+    pl.semaphore_wait(barrier, len(near))
+    for m in (sc_zu0, sc_xu1):
+        m.start()
+
+    known = [
+        near,
+        [at(**{a: d}) for a in AXES for d in (2, -2) if sizes[a] > 4 or (sizes[a] == 4 and d > 0)],
+        [at(gz=d) for d in (4, -4) if sizes["gz"] > 8] + [{"gz": me["gz"] + 1 - 2 * core}],
+    ]
+
+    def tell(i):
+        for other in known[i]:
+            pl.semaphore_signal(present.at[i], inc=1, device_id=other, device_id_type=MESH)
+
+    def told(i):
+        if known[i]:
+            pl.semaphore_wait(present.at[i], len(known[i]))
+
     arrived(2)
     for pair in loads[3:]:
         for copy in pair:
@@ -192,24 +210,7 @@
     load_ns.start()
     load_cs.start()
     ys_sc[2 * third :] = scale_all(2, jnp.zeros((L, L), F32), 0).T[:third]
-    pl.semaphore_wait(barrier, len(near))
-
-    known = [
-        near,
-        [at(**{a: d}) for a in AXES for d in (2, -2) if sizes[a] > 4 or (sizes[a] == 4 and d > 0)],
-        [at(gz=d) for d in (4, -4) if sizes["gz"] > 8] + [{"gz": me["gz"] + 1 - 2 * core}],
-    ]
-
-    def tell(i):
-        for other in known[i]:
-            pl.semaphore_signal(present.at[i], inc=1, device_id=other, device_id_type=MESH)
-
-    def told(i):
-        if known[i]:
-            pl.semaphore_wait(present.at[i], len(known[i]))
-
-    for m in (sc_yu2, sc_xu1, sc_zu0):
-        m.start()
+    sc_yu2.start()
     tell(0)
     arrived(3)
     packed = scale_all(1, jnp.zeros((L, L), F32), NB)

time: 32.5 us -> 32.5 us (level)
  no operation moved by 1% of the time
where the time goes in v8:
time: 32.5 us; the launch traced here: 32.4 us
  Pallas kernels  31.3 us (96%)
  local copies, waits for them, and re-layouts  1.15 us (4%)
    pallas_call x1, Pallas kernels, local(): pl.pallas_call(functools.partial(kernel, sizes), out_shape=jax.ShapeDtype...  31.3 us
    unnamed x1, local copies, waits for them, and re-layouts  1.15 us

profile of v8, /device:TPU:1, one launch (start us, length us, event | category | flops | bytes accessed | tf_op | source)
XLA Modules:
  0.0 32.4 jit_solution(6301134618593668523)
XLA Ops:
  0.0 31.3 %shard_map.46 = f32[3,16,64,128]{3,2,1,0:T(8,128)S(1)} custom-call(f32[3,16,64,128]{3,2,1,0:T(8,128)} %res_h.1, f32[3,16,64,128]{3,2,1,0:T(8,128)} %ed_h.1, f32[16,64,128]{2,1,0:T(8,128)} %ns_h.1, f32[8,32,64]{2,1,0:T(8,128)} %cs_h.1), custom_call_target="tpu_custom_call" | custom-call | tf_op jit(solution)/shard_map/pallas_call | solution.py:696
  31.3 1.1 %copy.6 = f32[3,16,64,128]{3,2,1,0:T(8,128)} copy(f32[3,16,64,128]{3,2,1,0:T(8,128)S(1)} %shard_map.46) | data formatting | bytes 3145728
